TPU v7x, 256 devices: a whole 4x4x8 slice. The times are simulated.
256 devices in a mesh: replica: 16 (over y_hi, x, core), model: 16 (over z, y_lo).
Axes of the slice: x: 4, y: 4 (y_hi: 2, y_lo: 2; y = y_hi * 2 + y_lo), z: 8, core: 2. Of those that a mesh axis runs over, the one named last changes fastest.
Arguments:
- slope_gate: float32 [16, 2048, 6144], P('replica', None, 'model'), may hold values from -0.875 to 0.875
- slope_up: float32 [16, 2048, 6144], P('replica', None, 'model'), may hold values from -0.875 to 0.875
- slope_down: float32 [16, 6144, 2048], P('replica', 'model'), may hold values from -0.875 to 0.875
- slope_norm: float32 [16, 2048], P('replica'), may hold values from -8 to 8
- param_gate: float32 [2048, 6144], P('replica', 'model'), may hold values from -0.1875 to 0.1875
- param_up: float32 [2048, 6144], P('replica', 'model'), may hold values from -0.1875 to 0.1875
- param_down: float32 [6144, 2048], P('model', 'replica'), may hold values from -0.109375 to 0.109375
- param_norm: float32 [2048], P('replica'), may hold values from 0.25 to 1.75
Outputs:
- half_gate: bfloat16 [2048, 6144], P(None, 'model')
- half_up: bfloat16 [2048, 6144], P(None, 'model')
- half_down: bfloat16 [6144, 2048], P('model')
- half_norm: bfloat16 [2048], replicated
- next_gate: float32 [2048, 6144], P('replica', 'model')
- next_up: float32 [2048, 6144], P('replica', 'model')
- next_down: float32 [6144, 2048], P('model', 'replica')
- next_norm: float32 [2048], P('replica')
All inputs are finite; a program needn't handle non-finite values.
Results may differ from a plain program's by a relative error of at most 0.0004.
Values may be sent and summed in bfloat16 or wider, within the bound.
A program may use at most 128 MiB of HBM per device.

v0:
```python
import jax
import jax.numpy as jnp
from jax import lax
from jax.sharding import Mesh
from jax.sharding import PartitionSpec as P

REPLICA = ("replica_0", "replica_1", "replica_2")


learn_rate = 0.5


def in_blocks(array, dim, devices):
    before, after = (array.shape[:dim], array.shape[dim + 1 :])
    return jnp.moveaxis(array.reshape(*before, devices, -1, *after), dim, 0)


def sum_at_owner(array, axis, dim):
    devices = lax.axis_size(axis)
    tiles = lax.all_to_all(in_blocks(array, dim, devices), axis, 0, 0, tiled=True)
    return jnp.sum(tiles, axis=0)


def sum_in_two_steps(array, axes, dim):
    far, near = axes
    own = sum_at_owner(in_blocks(array, dim, lax.axis_size(far)), near, dim + 1)
    return jnp.sum(lax.all_to_all(own, far, 0, 0, tiled=True), axis=0)


def sent_together(arrays, axis, dim, along):
    both = jnp.concatenate(arrays, axis=along)
    result, at, done = (sum_in_two_steps(both, axis, dim), 0, [])
    for a in arrays:
        done.append(lax.slice_in_dim(result, at, at + a.shape[along], axis=along))
        at += a.shape[along]
    return tuple(done)


def sent_to_all(array, axis):
    copies = jnp.broadcast_to(array, (lax.axis_size(axis), *array.shape))
    return lax.all_to_all(copies, axis, split_axis=0, concat_axis=0, tiled=True)


def taken_together(array, axis):
    return sent_to_all(array, axis).sum(axis=0)


def packed_total(arrays, axis):
    ends = [0]
    for a in arrays:
        ends.append(ends[-1] + a.size)
    total = taken_together(jnp.concatenate([a.ravel() for a in arrays]), axis)
    return tuple((total[b:e].reshape(a.shape) for a, b, e in zip(arrays, ends, ends[1:])))


def turned_gather(arrays, axis, dims):
    turned = [jnp.moveaxis(a, dim, 0) for a, dim in zip(arrays, dims)]
    both = jnp.concatenate([t.reshape(len(t), -1) for t in turned], axis=1)
    result, at, done = (lax.all_gather(both, axis, axis=0, tiled=True), 0, [])
    for t, dim in zip(turned, dims):
        share = result[:, at : at + t[0].size].reshape(-1, *t.shape[1:])
        done.append(jnp.moveaxis(share, 0, dim))
        at += t[0].size
    return tuple(done)


def body(
    slope_gate, slope_up, slope_down, slope_norm, param_gate, param_up, param_down, param_norm
):
    mean_gate, mean_up, mean_down, mean_norm = (
        *sent_together(
            (slope_gate[0], slope_up[0]), (("replica_0", "replica_1"), "replica_2"), 0, 1
        ),
        sum_in_two_steps(slope_down[0], (("replica_0", "replica_1"), "replica_2"), 1),
        sum_in_two_steps(slope_norm[0], (("replica_0", "replica_1"), "replica_2"), 0),
    )
    mean_rate = lax.axis_size(REPLICA) ** (-0.5)
    mean_gate = mean_gate * mean_rate
    mean_up = mean_up * mean_rate
    mean_down = mean_down * mean_rate
    mean_norm = mean_norm * mean_rate
    own_gate, own_up, own_down, slope_gate_norm, slope_up_norm, slope_down_norm = packed_total(
        (
            jnp.sum(param_gate * param_gate, axis=1, keepdims=True),
            jnp.sum(param_up * param_up, axis=1, keepdims=True),
            jnp.sum(param_down * param_down, axis=0, keepdims=True),
            jnp.sum(mean_gate * mean_gate, axis=1, keepdims=True),
            jnp.sum(mean_up * mean_up, axis=1, keepdims=True),
            jnp.sum(mean_down * mean_down, axis=0, keepdims=True),
        ),
        "model",
    )
    mean_gate = mean_gate * (jnp.sqrt(own_gate) * lax.rsqrt(slope_gate_norm + 1e-06))
    mean_up = mean_up * (jnp.sqrt(own_up) * lax.rsqrt(slope_up_norm + 1e-06))
    mean_down = mean_down * (jnp.sqrt(own_down) * lax.rsqrt(slope_down_norm + 1e-06))
    next_gate = param_gate - learn_rate * mean_gate
    next_up = param_up - learn_rate * mean_up
    next_down = param_down - learn_rate * mean_down
    next_norm = param_norm - learn_rate * mean_norm
    half_gate, half_up, half_down, half_norm = turned_gather(
        (
            next_gate.astype(jnp.bfloat16),
            next_up.astype(jnp.bfloat16),
            next_down.astype(jnp.bfloat16),
            next_norm.astype(jnp.bfloat16),
        ),
        REPLICA,
        (0, 0, 1, 0),
    )
    return (half_gate, half_up, half_down, half_norm, next_gate, next_up, next_down, next_norm)


def solution(mesh):
    finer = Mesh(
        mesh.devices.reshape(2, 4, 2, mesh.shape["model"]),
        ("replica_0", "replica_1", "replica_2", "model"),
    )
    placed = (
        P(REPLICA, None, "model"),
        P(REPLICA, None, "model"),
        P(REPLICA, "model", None),
        P(REPLICA, None),
        P(REPLICA, "model"),
        P(REPLICA, "model"),
        P("model", REPLICA),
        P(REPLICA),
    )
    return jax.shard_map(
        body,
        mesh=finer,
        in_specs=placed,
        out_specs=(
            P(None, "model"),
            P(None, "model"),
            P("model", None),
            P(),
            P(REPLICA, "model"),
            P(REPLICA, "model"),
            P("model", REPLICA),
            P(REPLICA),
        ),
        check_vma=False,
    )
```

profile of v0, /device:TPU:1, one launch (start us, length us, event | category | flops | bytes accessed | tf_op | source)
XLA Modules:
  0.0 234.4 jit_solution(9100243397128749743)
XLA Ops:
  8.5 6.4 %all-to-all-start.5 = ((f32[2,8,128]{2,1,0:T(8,128)}), f32[2,8,128]{2,1,0:T(8,128)S(1)}, u32[]{:S(2)}, u32[]{:S(2)}) async-start(f32[2,8,128]{2,1,0:T(8,128)} %copy.72), calls=%async_computation.5 | async-start | bytes 16384 | tf_op jit(solution)/shard_map/all_to_all | solution.py:20
  14.9 3.4 %maximum_bitcast_fusion = f32[2,8,128,768]{3,2,0,1:T(8,128)S(1)} fusion(f32[8,2,128,384]{3,2,1,0:T(8,128)} %bitcast.22, f32[8,2,128,384]{3,2,1,0:T(8,128)} %bitcast.23), kind=kLoop, calls=%fused_computation | loop fusion | flops 1572864 | bytes 12582912 | tf_op jit(solution)/shard_map/transpose | solution.py:15
  18.3 3.3 %copy.64 = f32[2,8,128,768]{3,2,1,0:T(8,128)} copy(f32[2,8,128,768]{3,2,0,1:T(8,128)S(1)} %maximum_bitcast_fusion) | data formatting | bytes 12582912 | tf_op jit(solution)/shard_map/transpose | solution.py:15
  21.7 2.4 %copy.65 = f32[1,384,2048]{1,2,0:T(8,128)} copy(f32[1,384,2048]{2,1,0:T(8,128)S(1)} %copy-done.1) | data formatting | bytes 6291456 | tf_op args[2]
  24.1 2.6 %copy.66 = f32[2,8,384,128]{3,1,2,0:T(8,128)S(1)} copy(f32[2,8,384,128]{2,3,0,1:T(8,128)} %bitcast.21) | data formatting | bytes 6291456 | tf_op jit(solution)/shard_map/transpose | solution.py:15
  26.7 6.3 %all-to-all-start = ((f32[2,8,128,768]{3,2,1,0:T(8,128)}), f32[2,8,128,768]{3,2,1,0:T(8,128)}, u32[]{:S(2)}, u32[]{:S(2)}) async-start(f32[2,8,128,768]{3,2,1,0:T(8,128)} %copy.64), calls=%async_computation | async-start | bytes 12582912 | tf_op jit(solution)/shard_map/all_to_all | solution.py:20
  33.6 5.0 %all-to-all-done = f32[2,8,128,768]{3,2,1,0:T(8,128)} async-done(((f32[2,8,128,768]{3,2,1,0:T(8,128)}), f32[2,8,128,768]{3,2,1,0:T(8,128)}, u32[]{:S(2)}, u32[]{:S(2)}) %all-to-all-start) | async-done | bytes 6291488 | tf_op jit(solution)/shard_map/all_to_all | solution.py:20
  38.6 7.2 %all_to_all.40 = f32[2,8,384,128]{3,1,2,0:T(8,128)} all-to-all(f32[2,8,384,128]{3,1,2,0:T(8,128)S(1)} %copy.66), channel_id=1, replica_groups=mesh['replica_0'=2,'replica_1'=4,'replica_2'=2,'model'=16] {'replica_2'}, dimensions={0} | all-to-all | bytes 6291456 | tf_op jit(solution)/shard_map/all_to_all | solution.py:20
  45.9 4.9 %all-to-all-start.6 = ((f32[8,1,128]{2,1,0:T(1,128)}), f32[8,1,128]{2,1,0:T(1,128)S(1)}, u32[]{:S(2)}, u32[]{:S(2)}) async-start(f32[8,1,128]{2,1,0:T(1,128)} %bitcast.10), calls=%async_computation.6 | async-start | bytes 8192 | tf_op jit(solution)/shard_map/all_to_all | solution.py:27
  50.8 2.3 reduce_sum.124
  54.5 2.8 %all-to-all-done.6 = f32[8,1,128]{2,1,0:T(1,128)S(1)} async-done(((f32[8,1,128]{2,1,0:T(1,128)}), f32[8,1,128]{2,1,0:T(1,128)S(1)}, u32[]{:S(2)}, u32[]{:S(2)}) %all-to-all-start.6) | async-done | bytes 4128 | tf_op jit(solution)/shard_map/all_to_all | solution.py:27
  57.3 3.9 %all-to-all-start.3 = ((f32[8,384,128]{2,1,0:T(8,128)}), f32[8,384,128]{2,1,0:T(8,128)S(1)}, u32[]{:S(2)}, u32[]{:S(2)}) async-start(f32[8,384,128]{2,1,0:T(8,128)} %copy.68), calls=%async_computation.3 | async-start | bytes 3145728 | tf_op jit(solution)/shard_map/all_to_all | solution.py:27
  61.1 5.3 %reduce_sum.117 = f32[8,128,768]{2,1,0:T(8,128)} reduce(f32[2,8,128,768]{3,2,1,0:T(8,128)} %all-to-all-done, f32[]{:T(128)} %constant.5.clone.1), dimensions={0}, to_apply=%region_0.0 | reduce | flops 786432 | bytes 9437188 | tf_op jit(solution)/shard_map/reduce_sum | solution.py:21
  66.4 17.7 %all-to-all-done.3 = f32[8,384,128]{2,1,0:T(8,128)S(1)} async-done(((f32[8,384,128]{2,1,0:T(8,128)}), f32[8,384,128]{2,1,0:T(8,128)S(1)}, u32[]{:S(2)}, u32[]{:S(2)}) %all-to-all-start.3) | async-done | bytes 1572896 | tf_op jit(solution)/shard_map/all_to_all | solution.py:27
  85.3 3.6 %all-to-all-start.1 = ((f32[8,128,768]{2,1,0:T(8,128)}), f32[8,128,768]{2,1,0:T(8,128)S(1)}, u32[]{:S(2)}, u32[]{:S(2)}) async-start(f32[8,128,768]{2,1,0:T(8,128)} %reduce_sum.117), calls=%async_computation.1 | async-start | bytes 6291456 | tf_op jit(solution)/shard_map/all_to_all | solution.py:27
  88.9 1.7 copy.71
  94.2 34.6 %all-to-all-done.1 = f32[8,128,768]{2,1,0:T(8,128)S(1)} async-done(((f32[8,128,768]{2,1,0:T(8,128)}), f32[8,128,768]{2,1,0:T(8,128)S(1)}, u32[]{:S(2)}, u32[]{:S(2)}) %all-to-all-start.1) | async-done | bytes 3145760 | tf_op jit(solution)/shard_map/all_to_all | solution.py:27
  129.7 8.4 %all-to-all-start.4 = ((f32[16,1,768]{2,1,0:T(1,128)}), f32[16,1,768]{2,1,0:T(1,128)S(1)}, u32[]{:S(2)}, u32[]{:S(2)}) async-start(f32[16,1,768]{2,1,0:T(1,128)} %broadcast_in_dim.3), calls=%async_computation.4 | async-start | bytes 98304 | tf_op jit(solution)/shard_map/all_to_all | solution.py:41
  139.9 6.0 %all-to-all-done.4 = f32[16,1,768]{2,1,0:T(1,128)S(1)} async-done(((f32[16,1,768]{2,1,0:T(1,128)}), f32[16,1,768]{2,1,0:T(1,128)S(1)}, u32[]{:S(2)}, u32[]{:S(2)}) %all-to-all-start.4) | async-done | bytes 49184 | tf_op jit(solution)/shard_map/all_to_all | solution.py:41
  146.0 1.9 fusion
  150.5 69.1 %all-gather.2.cloned.1.call-done = bf16[2048,1153]{1,0:T(8,128)(2,1)} async-done(((bf16[128,1153]{1,0:T(8,128)(2,1)}), bf16[2048,1153]{1,0:T(8,128)(2,1)}) %all-gather.2.cloned.1.call-update) | async-done | bytes 4722704 | tf_op jit(solution)/shard_map/all_gather | solution.py:59
  219.6 4.5 %slice_bitcast_fusion = (bf16[384,2048]{0,1:T(8,128)(2,1)S(1)}, bf16[2048,384]{1,0:T(8,128)(2,1)}, bf16[2048,384]{1,0:T(8,128)(2,1)}) fusion(bf16[2048,1153]{1,0:T(8,128)(2,1)} %all-gather.2.cloned.1.call-done), kind=kLoop, calls=%fused_computation.1 | loop fusion | bytes 9437184 | tf_op jit(solution)/shard_map/transpose | solution.py:62
  224.1 1.6 copy.74
  225.7 1.9 slice_reduce_fusion
  (42 shorter events, 13.3 us)
Async XLA Ops:
  8.5 18.2 %all-to-all-start.5 = ((f32[2,8,128]{2,1,0:T(8,128)}), f32[2,8,128]{2,1,0:T(8,128)S(1)}, u32[]{:S(2)}, u32[]{:S(2)}) async-start(f32[2,8,128]{2,1,0:T(8,128)} %copy.72), calls=%async_computation.5 | async-start | bytes 16384 | tf_op jit(solution)/shard_map/all_to_all | solution.py:20
  18.3 3.4 %copy-start.1 = (f32[1,384,2048]{2,1,0:T(8,128)S(1)}, f32[1,384,2048]{2,1,0:T(8,128)}, u32[]{:S(2)}) copy-start(f32[1,384,2048]{2,1,0:T(8,128)} %param.10) | copy-start | bytes 9437188
  26.7 12.0 %all-to-all-start = ((f32[2,8,128,768]{3,2,1,0:T(8,128)}), f32[2,8,128,768]{3,2,1,0:T(8,128)}, u32[]{:S(2)}, u32[]{:S(2)}) async-start(f32[2,8,128,768]{3,2,1,0:T(8,128)} %copy.64), calls=%async_computation | async-start | bytes 12582912 | tf_op jit(solution)/shard_map/all_to_all | solution.py:20
  45.9 11.4 %all-to-all-start.6 = ((f32[8,1,128]{2,1,0:T(1,128)}), f32[8,1,128]{2,1,0:T(1,128)S(1)}, u32[]{:S(2)}, u32[]{:S(2)}) async-start(f32[8,1,128]{2,1,0:T(1,128)} %bitcast.10), calls=%async_computation.6 | async-start | bytes 8192 | tf_op jit(solution)/shard_map/all_to_all | solution.py:27
  57.3 26.9 %all-to-all-start.3 = ((f32[8,384,128]{2,1,0:T(8,128)}), f32[8,384,128]{2,1,0:T(8,128)S(1)}, u32[]{:S(2)}, u32[]{:S(2)}) async-start(f32[8,384,128]{2,1,0:T(8,128)} %copy.68), calls=%async_computation.3 | async-start | bytes 3145728 | tf_op jit(solution)/shard_map/all_to_all | solution.py:27
  66.4 24.3 %copy-start.3 = (f32[128,384]{1,0:T(8,128)S(1)}, f32[128,384]{1,0:T(8,128)}, u32[]{:S(2)}) copy-start(f32[128,384]{1,0:T(8,128)} %param.12) | copy-start | bytes 589828
  66.4 24.4 %copy-start.4 = (f32[128,384]{1,0:T(8,128)S(1)}, f32[128,384]{1,0:T(8,128)}, u32[]{:S(2)}) copy-start(f32[128,384]{1,0:T(8,128)} %param.13) | copy-start | bytes 589828
  84.1 1.1 copy-start
  85.3 43.4 %all-to-all-start.1 = ((f32[8,128,768]{2,1,0:T(8,128)}), f32[8,128,768]{2,1,0:T(8,128)S(1)}, u32[]{:S(2)}, u32[]{:S(2)}) async-start(f32[8,128,768]{2,1,0:T(8,128)} %reduce_sum.117), calls=%async_computation.1 | async-start | bytes 6291456 | tf_op jit(solution)/shard_map/all_to_all | solution.py:27
  90.9 47.3 %copy-start.5 = (f32[128]{0:T(128)S(1)}, f32[128]{0:T(128)}, u32[]{:S(2)}) copy-start(f32[128]{0:T(128)} %param.15) | copy-start | bytes 1540
  93.5 0.7 copy-start.2
  129.7 16.2 %all-to-all-start.4 = ((f32[16,1,768]{2,1,0:T(1,128)}), f32[16,1,768]{2,1,0:T(1,128)S(1)}, u32[]{:S(2)}, u32[]{:S(2)}) async-start(f32[16,1,768]{2,1,0:T(1,128)} %broadcast_in_dim.3), calls=%async_computation.4 | async-start | bytes 98304 | tf_op jit(solution)/shard_map/all_to_all | solution.py:41
  138.1 81.5 %all-gather.2.cloned.1.call-start = ((), (), s32[]{:S(2)}) async-start(), calls=%async_computation.7 | async-start | bytes 5570560 | tf_op jit(solution)/shard_map/all_gather | solution.py:59
Sparse Core Ops, SparseCore 0:
  149.8 69.7 all-gather.1
where the time goes:
time: 235 us; the launch traced here: 234 us
  waiting for transfers between devices  135 us (57%)
  starting transfers between devices  33.7 us (14%)
  local copies, waits for them, and re-layouts  25.2 us (11%)
  other arithmetic  18.9 us (8%)
  between operations  14.2 us (6%)
  blocking collectives  7.21 us (3%)
    all_gather x1, waiting for transfers between devices, turned_gather(): result, at, done = (lax.all_gather(both, axis, axis=0, tiled=True), 0, [])  69.1 us
    all_to_all x3, waiting for transfers between devices, sum_in_two_steps(): return jnp.sum(lax.all_to_all(own, far, 0, 0, tiled=True), axis=0)  55 us
    all_to_all x2, starting transfers between devices, sum_at_owner(): lax.all_to_all(in_blocks(array, dim, devices), axis, 0, 0, tiled=True)  12.8 us
    all_to_all x3, starting transfers between devices, sum_in_two_steps(): return jnp.sum(lax.all_to_all(own, far, 0, 0, tiled=True), axis=0)  12.5 us
    all_to_all x1, starting transfers between devices, sent_to_all(): return lax.all_to_all(copies, axis, split_axis=0, concat_axis=0, tiled=True)  8.4 us
    unnamed x21, local copies, waits for them, and re-layouts  8.32 us
    reduce_sum x3, other arithmetic, sum_at_owner(): return jnp.sum(tiles, axis=0)  8.15 us
    transpose x3, local copies, waits for them, and re-layouts, in_blocks(): return jnp.moveaxis(array.reshape(*before, devices, -1, *after), dim, 0)  7.24 us
  transfers between devices with their start and end apart: 7, of which 6 were waited for; matrix products, arithmetic and copies ran while one was open for 12% of the time, Pallas kernels for 0%

commit v1 on v0

v1 whole, which is shorter than its diff:
```python
import functools

import jax
import jax.numpy as jnp
from jax import lax
from jax.experimental import pallas as pl
from jax.experimental.pallas import tpu as pltpu
from jax.sharding import PartitionSpec as P

MESH = pl.DeviceIdType.MESH
LEARN_RATE = 0.5
EPS = 1e-06
ROWS = 128
XS = 4


class Copies:
    def __init__(self, send, recv):
        self.send, self.recv, self.used, self.started = send, recv, 0, []

    def start(self, src, dst, target):
        copy = pltpu.make_async_remote_copy(
            src_ref=src,
            dst_ref=dst,
            send_sem=self.send.at[self.used],
            recv_sem=self.recv.at[self.used],
            device_id=target,
            device_id_type=MESH,
        )
        copy.start()
        self.used += 1
        self.started.append(copy)
        return copy

    def drain(self):
        for copy in self.started:
            copy.wait_send()


class Tensor:
    def __init__(self, by_rows, x_first, slope, param, half, new, scratch):
        self.by_rows, self.x_first = by_rows, x_first
        self.slope, self.param, self.half, self.new = slope, param, half, new
        (self.s, self.r, self.f, self.d, self.a, self.y, self.p, self.src, self.nm) = scratch
        self.block = self.p.shape

    def share(self, ref, index):
        at = pl.ds(pl.multiple_of(index * ROWS, ROWS), ROWS)
        return ref.at[at, :] if self.by_rows else ref.at[:, at]

    def part(self, ref, index, h):
        size = self.block[0] // 2
        if self.by_rows:
            return ref.at[pl.ds(pl.multiple_of(index * ROWS + h * size, size), size), :]
        return ref.at[pl.ds(h * size, size), pl.ds(pl.multiple_of(index * ROWS, ROWS), ROWS)]

    def item(self, yh, h, x):
        if self.x_first:
            return self.s.at[h, x]
        size = self.block[0] // 2
        return self.s.at[yh, x, pl.ds(h * size, size), :]

    def squares(self, value):
        value = value * value
        if not self.by_rows:
            return jnp.sum(value, axis=0, keepdims=True)
        folded = value[:, :ROWS]
        for at in range(ROWS, value.shape[1], ROWS):
            folded = folded + value[:, at : at + ROWS]
        return jnp.sum(folded.T, axis=0, keepdims=True)


def add(into, *others):
    value = into[...]
    for other in others:
        value = value + other[...]
    into[...] = value


def kernel(replicas, models, *refs):
    (sg, su, sd, sn, pg, pu, pd, pn), refs = refs[:8], refs[8:]
    (hg, hu, hd, hn, ng, nu, nd, nn), refs = refs[:8], refs[8:]
    ta, refs = Tensor(True, True, sg, pg, hg, ng, refs[:9]), refs[9:]
    ty, refs = Tensor(True, False, su, pu, hu, nu, refs[:9]), refs[9:]
    tb, refs = Tensor(False, True, sd, pd, hd, nd, refs[:9]), refs[9:]
    nv_src, nv_dst, nn_src, nn_dst, local_sem, send_sem, recv_sem = refs

    r = lax.axis_index("replica")
    m = lax.axis_index("model")
    core = r % 2
    x = (r // 2) % XS
    yh = r // (2 * XS)
    yo = 1 - yh
    xr, xl, x2 = (x + 1) % XS, (x + XS - 1) % XS, (x + 2) % XS

    def owner(y, xx, c):
        return (y * XS + xx) * 2 + c

    def device(y, xx, c):
        return {"replica": owner(y, xx, c), "model": m}

    right, left = device(yh, xr, core), device(yh, xl, core)
    across, partner = device(yo, x, core), device(yh, x, 1 - core)
    net = Copies(send_sem, recv_sem)

    order = [(ta, 0, x2), (ta, 1, x2), (ty, yo, x2), (ta, 1, xr), (ta, 0, xl), (ty, yo, xr)]
    order += [(ta, 0, xr), (ta, 1, xl), (ty, yo, xl), (tb, 0, x2), (tb, 1, x2)]
    order += [(ty, yh, x2), (ty, yh, xr), (ta, yo, x), (ta, yh, x), (tb, 1, xr), (tb, 0, xl)]
    order += [(ty, yh, xl), (ty, yo, x), (tb, 0, xr), (tb, 1, xl), (ty, yh, x)]
    order += [(tb, yo, x), (tb, yh, x)]
    loads = []
    for i, (t, y, xx) in enumerate(order):
        copy = pltpu.make_async_copy(
            t.share(t.slope.at[0], owner(y, xx, core)), t.s.at[y, xx], local_sem.at[i]
        )
        copy.start()
        loads.append(copy)
    params = []
    for i, t in enumerate((ta, ty, tb)):
        copy = pltpu.make_async_copy(t.param, t.p, local_sem.at[len(order) + i])
        copy.start()
        params.append(copy)
    for i in range(replicas):
        nv_src[i, 0:1, :] = sn[0:1, i * ROWS : (i + 1) * ROWS]

    barrier = pltpu.get_barrier_semaphore()
    peers = [{"replica": (r + k) % replicas, "model": m} for k in range(1, replicas)]
    others = [{"replica": r, "model": (m + k) % models} for k in range(1, models)]
    for peer in peers + others:
        pl.semaphore_signal(barrier, inc=1, device_id=peer, device_id_type=MESH)
    pl.semaphore_wait(barrier, replicas + models - 2)

    swaps = []
    for t, y, xx in order:
        swaps.append(
            net.start(t.share(t.slope.at[0], owner(y, xx, 1 - core)), t.r.at[y, xx], partner)
        )
    vectors = []
    for k, peer in enumerate(peers, 1):
        vectors.append(
            net.start(nv_src.at[peer["replica"], pl.ds(0, 1)], nv_dst.at[k, pl.ds(0, 1)], peer)
        )

    taken = [0]

    def take(count):
        for i in range(taken[0], taken[0] + count):
            t, y, xx = order[i]
            loads[i].wait()
            swaps[i].wait_recv()
            add(t.s.at[y, xx], t.r.at[y, xx])
        taken[0] += count

    def far(t):
        return (
            net.start(t.item(yh, 0, x2), t.f.at[0], right),
            net.start(t.item(yh, 1, x2), t.f.at[1], left),
        )

    def near(t):
        return (
            net.start(t.item(yh, 0, xl), t.d.at[0], left),
            net.start(t.item(yh, 1, xr), t.d.at[1], right),
        )

    def relay(t, got):
        got[0].wait_recv()
        add(t.item(yh, 0, xr), t.f.at[0])
        first = net.start(t.item(yh, 0, xr), t.a.at[0], right)
        got[1].wait_recv()
        add(t.item(yh, 1, xl), t.f.at[1])
        return first, net.start(t.item(yh, 1, xl), t.a.at[1], left)

    def settle(t, direct, relayed):
        for h in (0, 1):
            direct[h].wait_recv()
        for h in (0, 1):
            relayed[h].wait_recv()
            add(t.item(yh, h, x), t.d.at[h], t.a.at[h])

    def finish(t, extra=()):
        own = t.s.at[yh, x]
        value = own[...]
        for e in extra:
            value = value + e[...]
        value = value * (replicas**-0.5)
        own[...] = value
        t.src[0:1, :] = t.squares(value)
        sent = [
            net.start(t.src, t.nm.at[k], peer) for k, peer in enumerate(others, 1)
        ]
        return sent

    def update(t, sent):
        total = t.src[...]
        for copy in sent:
            copy.wait_recv()
        for k in range(1, models):
            total = total + t.nm[k]
        ratio = jnp.sqrt(total[1:2]) * lax.rsqrt(total[0:1] + EPS)
        if t.by_rows:
            ratio = jnp.broadcast_to(ratio, (ROWS, ROWS)).T
            ratio = jnp.concatenate([ratio] * (t.block[1] // ROWS), axis=1)
        new = t.p[...] - LEARN_RATE * (t.s[yh, x] * ratio)
        t.new[...] = new
        t.share(t.half, owner(yh, x, core))[...] = new.astype(jnp.bfloat16)

    def blk(t, y, xx):
        return t.share(t.half, owner(y, xx, core))

    def spread(t, y, xx, target):
        return net.start(blk(t, y, xx), blk(t, y, xx), target)

    handed = []

    def hand(t, y, xx):
        handed.append(spread(t, y, xx, partner))

    take(2)
    a_far = far(ta)
    take(1)
    y_got = [net.start(ty.s.at[yo, x2], ty.y.at[0], across)]
    take(2)
    a_near = near(ta)
    take(1)
    y_got.append(net.start(ty.s.at[yo, xr], ty.y.at[1], across))
    take(3)
    y_got.append(net.start(ty.s.at[yo, xl], ty.y.at[2], across))
    take(2)
    for t, copy in zip((ta, ty, tb), params):
        copy.wait()
        t.src[1:2, :] = t.squares(t.p[...])
    take(2)
    a_relay = relay(ta, a_far)
    b_far = far(tb)
    take(4)
    b_near = near(tb)
    take(7)

    mean = nv_src[r, 0:1, :]
    for k, copy in enumerate(vectors, 1):
        copy.wait_recv()
        mean = mean + nv_dst[k, 0:1, :]
    new = pn[...] - LEARN_RATE * (mean * (replicas**-0.5))
    nn[...] = new
    nn_src[0:1, :] = new
    nn_dst[r, 0:1, :] = new
    gathered = [
        net.start(nn_src.at[pl.ds(0, 1)], nn_dst.at[r, pl.ds(0, 1)], peer) for peer in peers
    ]

    y_got[0].wait_recv()
    add(ty.s.at[yh, x2], ty.y.at[0])
    y_got[1].wait_recv()
    add(ty.s.at[yh, xr], ty.y.at[1])
    settle(ta, a_near, a_relay)
    a_y = net.start(ta.s.at[yo, x], ta.y, across)
    y_got.append(net.start(ty.s.at[yo, x], ty.y.at[3], across))
    y_got[2].wait_recv()
    add(ty.s.at[yh, xl], ty.y.at[2])
    b_relay = relay(tb, b_far)
    y_far = far(ty)
    y_near = near(ty)
    a_y.wait_recv()
    a_norm = finish(ta, (ta.y,))
    y_got[3].wait_recv()
    add(ty.s.at[yh, x], ty.y.at[3])
    update(ta, a_norm)
    a_up = spread(ta, yh, x, across)
    hand(ta, yh, x)
    settle(tb, b_near, b_relay)
    b_y = net.start(tb.s.at[yo, x], tb.y, across)
    y_relay = relay(ty, y_far)
    a_own = (spread(ta, yh, x, right), spread(ta, yh, x, left))
    a_up.wait_recv()
    a_oth = (spread(ta, yo, x, right), spread(ta, yo, x, left))
    hand(ta, yo, x)
    settle(ty, y_near, y_relay)
    y_norm = finish(ty)
    b_y.wait_recv()
    b_norm = finish(tb, (tb.y,))

    def received(t, copy, y, xx):
        copy.wait_recv()
        hand(t, y, xx)

    received(ta, a_own[0], yh, xl)
    a_fwd0 = spread(ta, yh, xl, right)
    received(ta, a_own[1], yh, xr)
    received(ta, a_oth[1], yo, xr)
    a_fwd1 = spread(ta, yo, xr, left)
    received(ta, a_oth[0], yo, xl)

    update(ty, y_norm)
    y_own = (spread(ty, yh, x, right), spread(ty, yh, x, left))
    y_up = [spread(ty, yh, x, across)]
    hand(ty, yh, x)
    update(tb, b_norm)
    b_up = spread(tb, yh, x, across)
    b_own = (spread(tb, yh, x, right), spread(tb, yh, x, left))
    hand(tb, yh, x)
    received(ta, a_fwd0, yh, x2)
    received(ta, a_fwd1, yo, x2)

    y_own[0].wait_recv()
    part = ty.part(ty.half, owner(yh, xl, core), 0)
    y_fwd0 = net.start(part, part, right)
    y_up.append(spread(ty, yh, xl, across))
    y_own[1].wait_recv()
    part = ty.part(ty.half, owner(yh, xr, core), 1)
    y_fwd1 = net.start(part, part, left)
    y_up.append(spread(ty, yh, xr, across))
    b_up.wait_recv()
    b_oth = (spread(tb, yo, x, right), spread(tb, yo, x, left))
    hand(tb, yo, x)
    hand(ty, yh, xl)
    hand(ty, yh, xr)
    received(tb, b_own[0], yh, xl)
    b_fwd0 = spread(tb, yh, xl, right)
    received(tb, b_own[1], yh, xr)
    received(ty, y_up[0], yo, x)
    y_fwd0.wait_recv()
    y_fwd1.wait_recv()
    y_up.append(spread(ty, yh, x2, across))
    hand(ty, yh, x2)
    received(tb, b_oth[1], yo, xr)
    b_fwd1 = spread(tb, yo, xr, left)
    received(tb, b_oth[0], yo, xl)
    received(ty, y_up[1], yo, xl)
    received(ty, y_up[2], yo, xr)

    for copy in gathered:
        copy.wait_recv()
    for i in range(replicas):
        hn[i : i + 1, :] = nn_dst[i, 0:1, :]

    received(ty, y_up[3], yo, x2)
    received(tb, b_fwd0, yh, x2)
    received(tb, b_fwd1, yo, x2)
    for copy in handed:
        copy.wait_recv()
    net.drain()


def body(sg, su, sd, sn, pg, pu, pd, pn):
    replicas, models = lax.axis_size("replica"), lax.axis_size("model")
    width, cols = sg.shape[1:]
    f32, bf16 = jnp.float32, jnp.bfloat16

    def scratch(block, x_first):
        item = block if x_first else (block[0] // 2, block[1])
        return [
            pltpu.VMEM((2, XS, *block), f32),
            pltpu.VMEM((2, XS, *block), f32),
            pltpu.VMEM((2, *item), f32),
            pltpu.VMEM((2, *item), f32),
            pltpu.VMEM((2, *item), f32),
            pltpu.VMEM(block if x_first else (XS, *block), f32),
            pltpu.VMEM(block, f32),
            pltpu.VMEM((2, ROWS), f32),
            pltpu.VMEM((models, 2, ROWS), f32),
        ]

    vmem = pl.BlockSpec(memory_space=pltpu.VMEM)
    hbm = pl.BlockSpec(memory_space=pltpu.HBM)
    shape = jax.ShapeDtypeStruct
    out = pl.pallas_call(
        functools.partial(kernel, replicas, models),
        out_shape=(
            shape((width, cols), bf16),
            shape((width, cols), bf16),
            shape((cols, width), bf16),
            shape((replicas, ROWS), f32),
            shape((ROWS, cols), f32),
            shape((ROWS, cols), f32),
            shape((cols, ROWS), f32),
            shape((1, ROWS), f32),
        ),
        in_specs=[hbm, hbm, hbm, vmem, hbm, hbm, hbm, vmem],
        out_specs=(vmem,) * 8,
        scratch_shapes=[
            *scratch((ROWS, cols), True),
            *scratch((ROWS, cols), False),
            *scratch((cols, ROWS), True),
            pltpu.VMEM((replicas, 8, ROWS), f32),
            pltpu.VMEM((replicas, 8, ROWS), f32),
            pltpu.VMEM((8, ROWS), f32),
            pltpu.VMEM((replicas, 8, ROWS), f32),
            pltpu.SemaphoreType.DMA((27,)),
            pltpu.SemaphoreType.DMA((176,)),
            pltpu.SemaphoreType.DMA((176,)),
        ],
        compiler_params=pltpu.CompilerParams(
            collective_id=0, has_side_effects=True, vmem_limit_bytes=32 << 20
        ),
    )(sg, su, sd, sn, pg, pu, pd, pn.reshape(1, ROWS))
    hg, hu, hd, hn, ng, nu, nd, nn = out
    return hg, hu, hd, hn.reshape(-1).astype(bf16), ng, nu, nd, nn.reshape(ROWS)


def solution(mesh):
    return jax.shard_map(
        body,
        mesh=mesh,
        in_specs=(
            P("replica", None, "model"),
            P("replica", None, "model"),
            P("replica", "model", None),
            P("replica", None),
            P("replica", "model"),
            P("replica", "model"),
            P("model", "replica"),
            P("replica"),
        ),
        out_specs=(
            P(None, "model"),
            P(None, "model"),
            P("model", None),
            P(),
            P("replica", "model"),
            P("replica", "model"),
            P("model", "replica"),
            P("replica"),
        ),
        check_vma=False,
    )
```

time: 235 us -> 94.1 us (0.40)
  waiting for transfers between devices: 135 us -> 0 us
  Pallas kernels: 0 us -> 76.2 us
  starting transfers between devices: 33.7 us -> 0 us
  other arithmetic: 18.9 us -> 0.6 us
  between operations: 14.2 us -> 0.66 us
  local copies, waits for them, and re-layouts: 25.2 us -> 15.8 us
  blocking collectives: 7.21 us -> 0 us
    pallas_call x0 -> x1, Pallas kernels: none -> 76.2 us  [body(): pl.pallas_call(functools.partial(kernel, replicas, models), out_shape=(sh...]
    all_gather x1 -> x0, waiting for transfers between devices: 69.1 us -> none  [turned_gather(): result, at, done = (lax.all_gather(both, axis, axis=0, tiled=True), 0, [])]
    all_to_all x6 -> x0, waiting for transfers between devices: 66 us -> none  [the longest x3 55 us: sum_in_two_steps(): return jnp.sum(lax.all_to_all(own, far, 0, 0, tiled=True), axis=0)]
    all_to_all x6 -> x0, starting transfers between devices: 33.6 us -> none  [the longest x2 12.8 us: sum_at_owner(): lax.all_to_all(in_blocks(array, dim, devices), axis, 0, 0, tiled=True)]
    transpose x4 -> x0, local copies, waits for them, and re-layouts: 11.8 us -> none  [the longest x3 7.24 us: in_blocks(): return jnp.moveaxis(array.reshape(*before, devices, -1, *after), dim, 0)]
    reduce_sum x12 -> x0, other arithmetic: 11.3 us -> none  [the longest x3 8.15 us: sum_at_owner(): return jnp.sum(tiles, axis=0)]
    unnamed x21 -> x23, local copies, waits for them, and re-layouts: 8.32 us -> 15.8 us
    all_to_all x1 -> x0, blocking collectives: 7.21 us -> none  [sum_at_owner(): lax.all_to_all(in_blocks(array, dim, devices), axis, 0, 0, tiled=True)]
  transfers between devices with their start and end apart: 7 -> 0, of which waited for: 6 -> 0; matrix products, arithmetic and copies ran while one was open for 12% -> 0% of each run, Pallas kernels for 0% -> 0%
where the time goes in v1:
time: 94.1 us; the launch traced here: 93.2 us
  Pallas kernels  76.2 us (81%)
  local copies, waits for them, and re-layouts  15.8 us (17%)
    pallas_call x1, Pallas kernels, body(): pl.pallas_call(functools.partial(kernel, replicas, models), out_shape=(sh...  76.2 us
    unnamed x23, local copies, waits for them, and re-layouts  15.8 us

profile of v1, /device:TPU:1, one launch (start us, length us, event | category | flops | bytes accessed | tf_op | source)
XLA Modules:
  0.0 93.2 jit_solution(12187437173791013530)
XLA Ops:
  0.6 0.0 copy-start
  0.6 1.9 %copy-done = f32[1,2048,384]{2,1,0:T(8,128)S(1)} copy-done((f32[1,2048,384]{2,1,0:T(8,128)S(1)}, f32[1,2048,384]{2,1,0:T(8,128)}, u32[]{:S(2)}) %copy-start) | copy-done | bytes 3145752
  2.5 0.0 copy-start.1
  2.5 1.9 %copy-done.1 = f32[1,2048,384]{2,1,0:T(8,128)S(1)} copy-done((f32[1,2048,384]{2,1,0:T(8,128)S(1)}, f32[1,2048,384]{2,1,0:T(8,128)}, u32[]{:S(2)}) %copy-start.1) | copy-done | bytes 3145752
  4.4 0.0 copy-start.2
  4.4 1.9 %copy-done.2 = f32[1,384,2048]{2,1,0:T(8,128)S(1)} copy-done((f32[1,384,2048]{2,1,0:T(8,128)S(1)}, f32[1,384,2048]{2,1,0:T(8,128)}, u32[]{:S(2)}) %copy-start.2) | copy-done | bytes 3145752
  6.3 0.0 copy-start.3
  6.3 0.9 copy-done.3
  7.2 0.0 copy-start.4
  7.2 0.9 copy-done.4
  8.2 0.9 copy-done.5
  9.1 0.0 copy-start.6
  9.1 0.7 copy-done.6
  9.8 0.0 copy-start.7
  9.8 0.7 copy-done.7
  10.4 76.2 %shard_map.143 = (bf16[2048,384]{1,0:T(8,128)(2,1)S(1)}, bf16[2048,384]{1,0:T(8,128)(2,1)S(1)}, bf16[384,2048]{1,0:T(8,128)(2,1)S(1)}, f32[16,128]{1,0:T(8,128)S...) custom-call(f32[1,2048,384]{2,1,0:T(8,128)S(1)} %copy-done, ...), custom_call_target="tpu_custom_call" | custom-call | tf_op jit(solution)/shard_map/pallas_call | solution.py:367
  86.6 0.6 convert_bitcast_fusion
  87.2 1.1 %copy.23 = bf16[2048,384]{1,0:T(8,128)(2,1)} copy(bf16[2048,384]{1,0:T(8,128)(2,1)S(1)} %get-tuple-element.32) | data formatting | bytes 3145728
  88.3 1.1 %copy.24 = bf16[2048,384]{1,0:T(8,128)(2,1)} copy(bf16[2048,384]{1,0:T(8,128)(2,1)S(1)} %get-tuple-element.33) | data formatting | bytes 3145728
  89.5 1.1 %copy.25 = bf16[384,2048]{1,0:T(8,128)(2,1)} copy(bf16[384,2048]{1,0:T(8,128)(2,1)S(1)} %get-tuple-element.34) | data formatting | bytes 3145728
  90.6 0.7 copy.26
  91.3 0.7 copy.27
  92.0 0.7 copy.28
  92.7 0.5 copy.29
  (1 shorter events, 0.0 us)
Async XLA Ops:
  0.6 1.9 %copy-start = (f32[1,2048,384]{2,1,0:T(8,128)S(1)}, f32[1,2048,384]{2,1,0:T(8,128)}, u32[]{:S(2)}) copy-start(f32[1,2048,384]{2,1,0:T(8,128)} %refs_0_.1) | copy-start | bytes 9437188
  2.5 1.9 %copy-start.1 = (f32[1,2048,384]{2,1,0:T(8,128)S(1)}, f32[1,2048,384]{2,1,0:T(8,128)}, u32[]{:S(2)}) copy-start(f32[1,2048,384]{2,1,0:T(8,128)} %refs_1_.1) | copy-start | bytes 9437188
  4.4 1.9 %copy-start.2 = (f32[1,384,2048]{2,1,0:T(8,128)S(1)}, f32[1,384,2048]{2,1,0:T(8,128)}, u32[]{:S(2)}) copy-start(f32[1,384,2048]{2,1,0:T(8,128)} %refs_2_.1) | copy-start | bytes 9437188
  6.3 0.9 copy-start.3
  7.2 0.9 copy-start.4
  8.2 0.9 copy-start.5
  9.1 0.7 copy-start.6
  9.8 0.7 copy-start.7

commit v2 on v1

--- a/solution.py
+++ b/solution.py
@@ -83,7 +83,7 @@
     ta, refs = Tensor(True, True, sg, pg, hg, ng, refs[:9]), refs[9:]
     ty, refs = Tensor(True, False, su, pu, hu, nu, refs[:9]), refs[9:]
     tb, refs = Tensor(False, True, sd, pd, hd, nd, refs[:9]), refs[9:]
-    nv_src, nv_dst, nn_src, nn_dst, local_sem, send_sem, recv_sem = refs
+    nv_src, nv_dst, nn_src, nn_dst, pn_here, sn_here, local_sem, send_sem, recv_sem = refs
 
     r = lax.axis_index("replica")
     m = lax.axis_index("model")
@@ -120,14 +120,20 @@
         copy = pltpu.make_async_copy(t.param, t.p, local_sem.at[len(order) + i])
         copy.start()
         params.append(copy)
-    for i in range(replicas):
-        nv_src[i, 0:1, :] = sn[0:1, i * ROWS : (i + 1) * ROWS]
+    copy = pltpu.make_async_copy(pn, pn_here, local_sem.at[27])
+    copy.start()
+    params.append(copy)
+    small = pltpu.make_async_copy(sn, sn_here, local_sem.at[28])
+    small.start()
 
     barrier = pltpu.get_barrier_semaphore()
     peers = [{"replica": (r + k) % replicas, "model": m} for k in range(1, replicas)]
     others = [{"replica": r, "model": (m + k) % models} for k in range(1, models)]
     for peer in peers + others:
         pl.semaphore_signal(barrier, inc=1, device_id=peer, device_id_type=MESH)
+    small.wait()
+    for i in range(replicas):
+        nv_src[i, 0:1, :] = sn_here[0:1, i * ROWS : (i + 1) * ROWS]
     pl.semaphore_wait(barrier, replicas + models - 2)
 
     swaps = []
@@ -241,7 +247,8 @@
     for k, copy in enumerate(vectors, 1):
         copy.wait_recv()
         mean = mean + nv_dst[k, 0:1, :]
-    new = pn[...] - LEARN_RATE * (mean * (replicas**-0.5))
+    params[3].wait()
+    new = pn_here[...] - LEARN_RATE * (mean * (replicas**-0.5))
     nn[...] = new
     nn_src[0:1, :] = new
     nn_dst[r, 0:1, :] = new
@@ -332,7 +339,7 @@
     for copy in gathered:
         copy.wait_recv()
     for i in range(replicas):
-        hn[i : i + 1, :] = nn_dst[i, 0:1, :]
+        hn[i * ROWS : (i + 1) * ROWS] = nn_dst[i, 0, :].astype(jnp.bfloat16)
 
     received(ty, y_up[3], yo, x2)
     received(tb, b_fwd0, yh, x2)
@@ -342,7 +349,18 @@
     net.drain()
 
 
+def store(*refs):
+    copies = [
+        pltpu.make_async_copy(refs[i], refs[8 + i], refs[16].at[i]) for i in range(8)
+    ]
+    for copy in copies:
+        copy.start()
+    for copy in copies:
+        copy.wait()
+
+
 def body(sg, su, sd, sn, pg, pu, pd, pn):
+    arrays = (sg, su, sd, sn, pg, pu, pd, pn.reshape(1, ROWS))
     replicas, models = lax.axis_size("replica"), lax.axis_size("model")
     width, cols = sg.shape[1:]
     f32, bf16 = jnp.float32, jnp.bfloat16
@@ -370,13 +388,13 @@
             shape((width, cols), bf16),
             shape((width, cols), bf16),
             shape((cols, width), bf16),
-            shape((replicas, ROWS), f32),
+            shape((width,), bf16),
             shape((ROWS, cols), f32),
             shape((ROWS, cols), f32),
             shape((cols, ROWS), f32),
             shape((1, ROWS), f32),
         ),
-        in_specs=[hbm, hbm, hbm, vmem, hbm, hbm, hbm, vmem],
+        in_specs=[hbm] * 8,
         out_specs=(vmem,) * 8,
         scratch_shapes=[
             *scratch((ROWS, cols), True),
@@ -386,16 +404,26 @@
             pltpu.VMEM((replicas, 8, ROWS), f32),
             pltpu.VMEM((8, ROWS), f32),
             pltpu.VMEM((replicas, 8, ROWS), f32),
-            pltpu.SemaphoreType.DMA((27,)),
+            pltpu.VMEM((1, ROWS), f32),
+            pltpu.VMEM((1, width), f32),
+            pltpu.SemaphoreType.DMA((29,)),
             pltpu.SemaphoreType.DMA((176,)),
             pltpu.SemaphoreType.DMA((176,)),
         ],
         compiler_params=pltpu.CompilerParams(
             collective_id=0, has_side_effects=True, vmem_limit_bytes=32 << 20
         ),
-    )(sg, su, sd, sn, pg, pu, pd, pn.reshape(1, ROWS))
-    hg, hu, hd, hn, ng, nu, nd, nn = out
-    return hg, hu, hd, hn.reshape(-1).astype(bf16), ng, nu, nd, nn.reshape(ROWS)
+    )(*(pltpu.with_memory_space_constraint(a, pltpu.HBM) for a in arrays))
+    out = (*out[:3], out[3].reshape(width), *out[4:])
+    out = pl.pallas_call(
+        store,
+        out_shape=tuple(shape(o.shape, o.dtype) for o in out),
+        in_specs=[vmem] * 8,
+        out_specs=(hbm,) * 8,
+        scratch_shapes=[pltpu.SemaphoreType.DMA((8,))],
+        compiler_params=pltpu.CompilerParams(vmem_limit_bytes=8 << 20),
+    )(*(pltpu.with_memory_space_constraint(o, pltpu.VMEM) for o in out))
+    return (*out[:7], out[7].reshape(ROWS))
 
 
 def solution(mesh):

time: 94.1 us -> 75.2 us (0.80)
  local copies, waits for them, and re-layouts: 15.8 us -> 0 us
  Pallas kernels: 76.2 us -> 73.9 us
    unnamed x23 -> x0, local copies, waits for them, and re-layouts: 15.8 us -> none
    pallas_call x1, Pallas kernels: 76.2 us -> 71.5 us  [body(): pl.pallas_call(functools.partial(kernel, replicas, models), out_shape=(sh...]
    pallas_call x0 -> x1, Pallas kernels: none -> 2.43 us  [body(): pl.pallas_call(store, out_shape=tuple((shape(o.shape, o.dtype) for o in o...]
where the time goes in v2:
time: 75.2 us; the launch traced here: 74.6 us
  Pallas kernels  73.9 us (98%)
    pallas_call x1, Pallas kernels, body(): pl.pallas_call(functools.partial(kernel, replicas, models), out_shape=(sh...  71.5 us
    pallas_call x1, Pallas kernels, body(): pl.pallas_call(store, out_shape=tuple((shape(o.shape, o.dtype) for o in o...  2.43 us

profile of v2, /device:TPU:1, one launch (start us, length us, event | category | flops | bytes accessed | tf_op | source)
XLA Modules:
  0.0 74.6 jit_solution(13224984537211694616)
XLA Ops:
  0.6 71.5 %shard_map.143 = (bf16[2048,384]{1,0:T(8,128)(2,1)S(1)}, bf16[2048,384]{1,0:T(8,128)(2,1)S(1)}, bf16[384,2048]{1,0:T(8,128)(2,1)S(1)}, bf16[2048]{0:T(1024)(128)...) custom-call(f32[1,2048,384]{2,1,0:T(8,128)} %refs_0_.1, ...), custom_call_target="tpu_custom_call" | custom-call | tf_op jit(solution)/shard_map/pallas_call | solution.py:385
  72.1 2.4 %shard_map.144 = (bf16[2048,384]{1,0:T(8,128)(2,1)}, bf16[2048,384]{1,0:T(8,128)(2,1)}, bf16[384,2048]{1,0:T(8,128)(2,1)}, bf16[2048]{0:T(1024)(128)(2,1)}, f32[...) custom-call(bf16[2048,384]{1,0:T(8,128)(2,1)S(1)} %get-tuple-element.24.refs_0_, ...), custom_call_target="tpu_custom_call" | custom-call | tf_op jit(solution)/shard_map/pallas_call | solution.py:418

commit v3 on v2

v3 whole, which is shorter than its diff:
```python
import functools

import jax
import jax.numpy as jnp
from jax import lax
from jax.experimental import pallas as pl
from jax.experimental.pallas import tpu as pltpu
from jax.sharding import PartitionSpec as P

MESH = pl.DeviceIdType.MESH
LEARN_RATE = 0.5
EPS = 1e-06
ROWS = 128
XS = 4


class Copies:
    def __init__(self, send, recv):
        self.send, self.recv, self.used, self.started = send, recv, 0, []
        self.drained = 0

    def start(self, src, dst, target):
        copy = pltpu.make_async_remote_copy(
            src_ref=src,
            dst_ref=dst,
            send_sem=self.send.at[self.used],
            recv_sem=self.recv.at[self.used],
            device_id=target,
            device_id_type=MESH,
        )
        copy.start()
        self.used += 1
        self.started.append(copy)
        return copy

    def mark(self):
        return len(self.started)

    def drain(self, upto):
        for copy in self.started[self.drained : upto]:
            copy.wait_send()
        self.drained = max(self.drained, upto)


class Matrix:
    def __init__(self, by_rows, slope, param, half, new, s, r, p):
        self.by_rows, self.slope, self.param, self.half, self.new = by_rows, slope, param, half, new
        self.s, self.r, self.p = s, r, p

    def share(self, ref, index):
        at = pl.ds(pl.multiple_of(index * ROWS, ROWS), ROWS)
        return ref.at[at, :] if self.by_rows else ref.at[:, at]


class Tensor:
    def __init__(self, whole, x_first, low, rows, f, d, a, y, src, nm):
        self.whole, self.x_first, self.low, self.rows = whole, x_first, low, rows
        self.f, self.d, self.a, self.y, self.src, self.nm = f, d, a, y, src, nm
        self.by_rows = whole.by_rows
        self.p = whole.p.at[pl.ds(low, rows)]
        self.new = whole.new.at[pl.ds(low, rows)]

    def sums(self, y, x):
        return self.whole.s.at[y, x, pl.ds(self.low, self.rows)]

    def block(self, index):
        return self.part(index, 0, self.rows)

    def part(self, index, at, rows):
        at = self.low + at
        if self.by_rows:
            at = pl.ds(pl.multiple_of(index * ROWS + at, rows), rows)
            return self.whole.half.at[at, :]
        return self.whole.half.at[pl.ds(at, rows), pl.ds(pl.multiple_of(index * ROWS, ROWS), ROWS)]

    def item(self, yh, h, x):
        if self.x_first:
            return self.sums(h, x)
        size = self.rows // 2
        return self.whole.s.at[yh, x, pl.ds(self.low + h * size, size)]

    def squares(self, value):
        value = value * value
        if not self.by_rows:
            return jnp.sum(value, axis=0, keepdims=True)
        folded = value[:, :ROWS]
        for at in range(ROWS, value.shape[1], ROWS):
            folded = folded + value[:, at : at + ROWS]
        if self.rows < ROWS:
            folded = jnp.concatenate([folded, jnp.zeros_like(folded)], axis=0)
        return jnp.sum(folded.T, axis=0, keepdims=True)


class Vector:
    x_first = True

    def __init__(self, s, f, d, a, y):
        self.s, self.f, self.d, self.a, self.y = s, f, d, a, y

    def item(self, yh, h, x):
        return self.s.at[h, x]


def add(into, *others):
    value = into[...]
    for other in others:
        value = value + other[...]
    into[...] = value


def kernel(replicas, models, *refs):
    (sg, su, sd, sn, pg, pu, pd, pn), refs = refs[:8], refs[8:]
    (hg, hu, hd, hn, ng, nu, nd, nn), refs = refs[:8], refs[8:]
    my, refs = Matrix(True, sg, pg, hg, ng, *refs[:3]), refs[3:]
    mb, refs = Matrix(True, su, pu, hu, nu, *refs[:3]), refs[3:]
    ma, refs = Matrix(False, sd, pd, hd, nd, *refs[:3]), refs[3:]
    half = ROWS // 2
    ta, refs = Tensor(ma, True, 0, ma.p.shape[0], *refs[:6]), refs[6:]
    b1, refs = Tensor(mb, True, 0, half, *refs[:6]), refs[6:]
    b2, refs = Tensor(mb, True, half, half, *refs[:6]), refs[6:]
    y1, refs = Tensor(my, False, 0, half, *refs[:3], None, *refs[3:5]), refs[5:]
    y2, refs = Tensor(my, False, half, half, *refs[:3], None, *refs[3:5]), refs[5:]
    y_in, refs = refs[0], refs[1:]
    tn, refs = Vector(*refs[:5]), refs[5:]
    gain, pn_here, sn_here, sn_other, local_sem, send_sem, recv_sem, hop_sem = refs

    r = lax.axis_index("replica")
    m = lax.axis_index("model")
    core = r % 2
    x = (r // 2) % XS
    yh = r // (2 * XS)
    yo = 1 - yh
    xr, xl, x2 = (x + 1) % XS, (x + XS - 1) % XS, (x + 2) % XS

    def owner(y, xx, c):
        return (y * XS + xx) * 2 + c

    def device(y, xx, c):
        return {"replica": owner(y, xx, c), "model": m}

    right, left = device(yh, xr, core), device(yh, xl, core)
    across, partner = device(yo, x, core), device(yh, x, 1 - core)
    net = Copies(send_sem, recv_sem)
    others = [{"replica": r, "model": (m + k) % models} for k in range(1, models)]
    zs = models // 2
    z, yl = m // 2, m % 2
    up = {"replica": r, "model": (z + 1) % zs * 2 + yl}
    down = {"replica": r, "model": (z + zs - 1) % zs * 2 + yl}
    beside = {"replica": r, "model": z * 2 + 1 - yl}

    def signal(sem, *peers):
        for peer in peers:
            pl.semaphore_signal(sem, inc=1, device_id=peer, device_id_type=MESH)

    barrier = pltpu.get_barrier_semaphore()
    signal(barrier, partner, right, left, across, up, down, beside)

    order = [("af", ma, 0, x2), ("af", ma, 1, x2), ("y0", my, yo, x2)]
    order += [("an", ma, 1, xr), ("an", ma, 0, xl), ("y1", my, yo, xr)]
    order += [("ar", ma, 0, xr), ("ar", ma, 1, xl), ("y2", my, yo, xl)]
    order += [("bf", mb, 0, x2), ("bf", mb, 1, x2), ("y3", my, yo, x)]
    order += [("yx2", my, yh, x2), ("bn", mb, 1, xr), ("bn", mb, 0, xl)]
    order += [("br", mb, 0, xr), ("br", mb, 1, xl), ("yx", my, yh, xr)]
    order += [("yx", my, yh, xl), ("ao", ma, 0, x), ("ao", ma, 1, x)]
    order += [("bo", mb, 0, x), ("bo", mb, 1, x), ("yo", my, yh, x)]
    loads = []
    for i, (_, t, y, xx) in enumerate(order):
        copy = pltpu.make_async_copy(
            t.share(t.slope.at[0], owner(y, xx, core)), t.s.at[y, xx], local_sem.at[i]
        )
        copy.start()
        loads.append(copy)
    params = []
    for i, t in enumerate((ma, mb, my)):
        copy = pltpu.make_async_copy(t.param, t.p, local_sem.at[len(order) + i])
        copy.start()
        params.append(copy)
    copy = pltpu.make_async_copy(pn, pn_here, local_sem.at[27])
    copy.start()
    params.append(copy)
    small = pltpu.make_async_copy(sn, sn_here, local_sem.at[28])
    small.start()
    pl.semaphore_wait(barrier, 7)

    swaps = []
    for tag, t, y, xx in order:
        swaps.append(
            net.start(t.share(t.slope.at[0], owner(y, xx, 1 - core)), t.r.at[y, xx], partner)
        )
        if tag == "y2":
            small_swap = net.start(sn, sn_other, partner)
            signal(hop_sem.at[0], up, down)
    swapped = net.mark()

    taken = [0]

    def take(tag):
        end = max(i for i, entry in enumerate(order) if entry[0] == tag) + 1
        for i in range(taken[0], end):
            _, t, y, xx = order[i]
            loads[i].wait()
            swaps[i].wait_recv()
            add(t.s.at[y, xx], t.r.at[y, xx])
        taken[0] = max(taken[0], end)

    def far(t):
        return (
            net.start(t.item(yh, 0, x2), t.f.at[0], right),
            net.start(t.item(yh, 1, x2), t.f.at[1], left),
        )

    def near(t):
        return (
            net.start(t.item(yh, 0, xl), t.d.at[0], left),
            net.start(t.item(yh, 1, xr), t.d.at[1], right),
        )

    def relay(t, got):
        got[0].wait_recv()
        add(t.item(yh, 0, xr), t.f.at[0])
        first = net.start(t.item(yh, 0, xr), t.a.at[0], right)
        got[1].wait_recv()
        add(t.item(yh, 1, xl), t.f.at[1])
        return first, net.start(t.item(yh, 1, xl), t.a.at[1], left)

    def settle(t, direct, relayed):
        for h in (0, 1):
            direct[h].wait_recv()
        for h in (0, 1):
            relayed[h].wait_recv()
            add(t.item(yh, h, x), t.d.at[h], t.a.at[h])

    def finish(t, extra=()):
        own = t.sums(yh, x)
        value = own[...]
        for e in extra:
            value = value + e[...]
        value = value * (replicas**-0.5)
        own[...] = value
        t.src[0:1, :] = t.squares(value)
        return [net.start(t.src, t.nm.at[k], peer) for k, peer in enumerate(others, 1)]

    def update(t, sent):
        total = t.src[...]
        for copy in sent:
            copy.wait_recv()
        for k in range(1, models):
            total = total + t.nm[k]
        ratio = jnp.sqrt(total[1:2]) * lax.rsqrt(total[0:1] + EPS)
        if t.by_rows:
            ratio = jnp.broadcast_to(ratio, (ROWS, ROWS)).T[: t.rows]
            ratio = jnp.concatenate([ratio] * (t.p.shape[1] // ROWS), axis=1)
        new = t.p[...] - LEARN_RATE * (t.sums(yh, x)[...] * ratio)
        t.new[...] = new
        t.block(owner(yh, x, core))[...] = new.astype(jnp.bfloat16)

    def spread(t, y, xx, target):
        block = t.block(owner(y, xx, core))
        return net.start(block, block, target)

    handed = []

    def hand(t, y, xx):
        handed.append(spread(t, y, xx, partner))

    def received(t, copy, y, xx):
        copy.wait_recv()
        hand(t, y, xx)

    def both(t, y):
        return spread(t, y, x, right), spread(t, y, x, left)

    def fold(got, xx, j):
        got.wait_recv()
        add(my.s.at[yh, xx], y_in.at[j])

    take("af")
    a_far = far(ta)
    take("y0")
    y_got = [net.start(my.s.at[yo, x2], y_in.at[0], across)]
    take("an")
    a_near = near(ta)
    take("y1")
    y_got.append(net.start(my.s.at[yo, xr], y_in.at[1], across))
    take("ar")
    take("y2")
    y_got.append(net.start(my.s.at[yo, xl], y_in.at[2], across))
    for copy in params[:3]:
        copy.wait()
    for t in (ta, b1, b2, y1, y2):
        t.src[1:2, :] = t.squares(t.p[...])
    small.wait()
    small_swap.wait_recv()
    for y in (0, 1):
        for xx in range(XS):
            at = pl.ds(pl.multiple_of(owner(y, xx, core) * ROWS, ROWS), ROWS)
            tn.s[y, xx] = sn_here[0:1, at] + sn_other[0:1, at]
    n_far = far(tn)
    n_near = near(tn)
    take("bf")
    pl.semaphore_wait(hop_sem.at[0], 2)
    signal(hop_sem.at[1], up, down)
    take("yx2")
    a_relay = relay(ta, a_far)
    take("bn")
    fold(y_got[0], x2, 0)
    pl.semaphore_wait(hop_sem.at[1], 2)
    signal(hop_sem.at[2], up, down)
    take("yo")
    n_relay = relay(tn, n_far)
    b1_far, b2_far = far(b1), far(b2)
    b1_near = near(b1)
    pl.semaphore_wait(hop_sem.at[2], 2)
    signal(hop_sem.at[3], beside)
    fold(y_got[1], xr, 1)
    net.drain(swapped)
    settle(ta, a_near, a_relay)
    a_y = net.start(ta.sums(yo, x), ta.y, across)
    y_got.append(net.start(my.s.at[yo, x], y_in.at[3], across))
    settle(tn, n_near, n_relay)
    n_y = net.start(tn.s.at[yo, x], tn.y, across)
    fold(y_got[2], xl, 2)
    b1_relay = relay(b1, b1_far)
    b2_near = near(b2)
    b2_relay = relay(b2, b2_far)
    y1_far, y2_far = far(y1), far(y2)
    y1_near, y2_near = near(y1), near(y2)
    pl.semaphore_wait(hop_sem.at[3], 1)
    mark = net.mark() - 16
    net.drain(mark)
    a_y.wait_recv()
    a_norm = finish(ta, (ta.y,))
    settle(b1, b1_near, b1_relay)
    b1_y = net.start(b1.sums(yo, x), b1.y, across)
    n_y.wait_recv()
    params[3].wait()
    add(tn.s.at[yh, x], tn.y)
    gain[core, yh * XS + x] = pn_here[...] - LEARN_RATE * (tn.s[yh, x] * (replicas**-0.5))
    nn[...] = gain[core, yh * XS + x]

    def tell(y, xx, target):
        row = gain.at[core, y * XS + xx]
        return net.start(row, row, target)

    n_up = tell(yh, x, across)
    fold(y_got[3], x, 3)
    update(ta, a_norm)
    a_up = spread(ta, yh, x, across)
    hand(ta, yh, x)
    settle(b2, b2_near, b2_relay)
    b2_y = net.start(b2.sums(yo, x), b2.y, across)
    y1_relay = relay(y1, y1_far)
    b1_y.wait_recv()
    b1_norm = finish(b1, (b1.y,))
    y2_relay = relay(y2, y2_far)
    n_own = (tell(yh, x, right), tell(yh, x, left))
    n_up.wait_recv()
    n_oth = (tell(yo, x, right), tell(yo, x, left))
    a_own = both(ta, yh)
    net.drain(net.mark() - 32)
    settle(y1, y1_near, y1_relay)
    y1_norm = finish(y1)
    a_up.wait_recv()
    a_oth = both(ta, yo)
    hand(ta, yo, x)
    b2_y.wait_recv()
    b2_norm = finish(b2, (b2.y,))
    update(b1, b1_norm)
    b1_up = spread(b1, yh, x, across)
    b1_own = both(b1, yh)
    hand(b1, yh, x)
    settle(y2, y2_near, y2_relay)
    y2_norm = finish(y2)
    n_own[0].wait_recv()
    n_fwd0 = tell(yh, xl, right)
    n_own[1].wait_recv()
    n_oth[0].wait_recv()
    n_oth[1].wait_recv()
    n_fwd1 = tell(yo, xr, left)
    received(ta, a_own[0], yh, xl)
    a_fwd0 = spread(ta, yh, xl, right)
    received(ta, a_own[1], yh, xr)
    update(y1, y1_norm)
    y1_own = both(y1, yh)
    y1_up = [spread(y1, yh, x, across)]
    hand(y1, yh, x)
    received(ta, a_oth[1], yo, xr)
    a_fwd1 = spread(ta, yo, xr, left)
    update(b2, b2_norm)
    b2_up = spread(b2, yh, x, across)
    update(y2, y2_norm)
    y2_own = both(y2, yh)
    b2_own = both(b2, yh)
    y2_up = [spread(y2, yh, x, across)]
    hand(b2, yh, x)
    hand(y2, yh, x)
    b1_up.wait_recv()
    b1_oth = both(b1, yo)
    received(ta, a_oth[0], yo, xl)
    hand(b1, yo, x)
    received(b1, b1_own[0], yh, xl)
    b1_fwd0 = spread(b1, yh, xl, right)
    received(b1, b1_own[1], yh, xr)
    n_fwd0.wait_recv()
    n_fwd1.wait_recv()
    n_hand = net.start(gain.at[core], gain.at[core], partner)
    net.drain(net.mark() - 32)

    def pass_on(t, own, ups):
        own[0].wait_recv()
        part = t.part(owner(yh, xl, core), 0, t.rows // 2)
        first = net.start(part, part, right)
        own[1].wait_recv()
        part = t.part(owner(yh, xr, core), t.rows // 2, t.rows // 2)
        second = net.start(part, part, left)
        ups.append(spread(t, yh, xl, across))
        ups.append(spread(t, yh, xr, across))
        hand(t, yh, xl)
        hand(t, yh, xr)
        return first, second

    def last_up(t, passed, ups):
        passed[0].wait_recv()
        passed[1].wait_recv()
        ups.append(spread(t, yh, x2, across))
        hand(t, yh, x2)

    y1_fwd = pass_on(y1, y1_own, y1_up)
    b2_up.wait_recv()
    b2_oth = both(b2, yo)
    hand(b2, yo, x)
    y2_fwd = pass_on(y2, y2_own, y2_up)
    received(b2, b2_own[0], yh, xl)
    b2_fwd0 = spread(b2, yh, xl, right)
    received(b2, b2_own[1], yh, xr)
    received(b1, b1_oth[1], yo, xr)
    b1_fwd1 = spread(b1, yo, xr, left)
    last_up(y1, y1_fwd, y1_up)
    received(b1, b1_oth[0], yo, xl)
    received(ta, a_fwd0, yh, x2)
    received(ta, a_fwd1, yo, x2)
    n_hand.wait_recv()
    for y in (0, 1):
        for xx in range(XS):
            for c in (0, 1):
                at = owner(y, xx, c) * ROWS
                hn[at : at + ROWS] = gain[c, y * XS + xx, 0, :].astype(jnp.bfloat16)
    received(b2, b2_oth[1], yo, xr)
    b2_fwd1 = spread(b2, yo, xr, left)
    last_up(y2, y2_fwd, y2_up)
    received(b2, b2_oth[0], yo, xl)
    received(y1, y1_up[0], yo, x)
    received(y2, y2_up[0], yo, x)
    received(b1, b1_fwd0, yh, x2)
    received(y1, y1_up[1], yo, xl)
    received(y1, y1_up[2], yo, xr)
    received(b1, b1_fwd1, yo, x2)
    early = len(handed) - 10
    for copy in handed[:early]:
        copy.wait_recv()
    net.drain(net.mark() - 16)
    received(y2, y2_up[1], yo, xl)
    received(y2, y2_up[2], yo, xr)
    received(b2, b2_fwd0, yh, x2)
    received(y1, y1_up[3], yo, x2)
    received(b2, b2_fwd1, yo, x2)
    received(y2, y2_up[3], yo, x2)
    for copy in handed[early:]:
        copy.wait_recv()
    net.drain(net.mark())


def store(*refs):
    copies = [
        pltpu.make_async_copy(refs[i], refs[8 + i], refs[16].at[i]) for i in range(8)
    ]
    for copy in copies:
        copy.start()
    for copy in copies:
        copy.wait()


def body(sg, su, sd, sn, pg, pu, pd, pn):
    arrays = (sg, su, sd, sn, pg, pu, pd, pn.reshape(1, ROWS))
    replicas, models = lax.axis_size("replica"), lax.axis_size("model")
    width, cols = sg.shape[1:]
    f32, bf16 = jnp.float32, jnp.bfloat16

    def matrix(share):
        sums = pltpu.VMEM((2, XS, *share), f32)
        return [sums, sums, pltpu.VMEM(share, f32)]

    def scratch(block, x_first):
        item = block if x_first else (block[0] // 2, block[1])
        arrived = [pltpu.VMEM((2, *item), f32)] * 3 + [pltpu.VMEM(block, f32)] * x_first
        return arrived + [pltpu.VMEM((2, ROWS), f32), pltpu.VMEM((models, 2, ROWS), f32)]

    vmem = pl.BlockSpec(memory_space=pltpu.VMEM)
    hbm = pl.BlockSpec(memory_space=pltpu.HBM)
    shape = jax.ShapeDtypeStruct
    out = pl.pallas_call(
        functools.partial(kernel, replicas, models),
        out_shape=(
            shape((width, cols), bf16),
            shape((width, cols), bf16),
            shape((cols, width), bf16),
            shape((width,), bf16),
            shape((ROWS, cols), f32),
            shape((ROWS, cols), f32),
            shape((cols, ROWS), f32),
            shape((1, ROWS), f32),
        ),
        in_specs=[hbm] * 8,
        out_specs=(vmem,) * 8,
        scratch_shapes=[
            *matrix((ROWS, cols)),
            *matrix((ROWS, cols)),
            *matrix((cols, ROWS)),
            *scratch((cols, ROWS), True),
            *scratch((ROWS // 2, cols), True),
            *scratch((ROWS // 2, cols), True),
            *scratch((ROWS // 2, cols), False),
            *scratch((ROWS // 2, cols), False),
            pltpu.VMEM((XS, ROWS, cols), f32),
            pltpu.VMEM((2, XS, 1, ROWS), f32),
            *[pltpu.VMEM((2, 1, ROWS), f32)] * 3,
            pltpu.VMEM((1, ROWS), f32),
            pltpu.VMEM((2, 2 * XS, 1, ROWS), f32),
            pltpu.VMEM((1, ROWS), f32),
            pltpu.VMEM((1, width), f32),
            pltpu.VMEM((1, width), f32),
            pltpu.SemaphoreType.DMA((29,)),
            pltpu.SemaphoreType.DMA((256,)),
            pltpu.SemaphoreType.DMA((256,)),
            pltpu.SemaphoreType.REGULAR((4,)),
        ],
        compiler_params=pltpu.CompilerParams(
            collective_id=0, has_side_effects=True, vmem_limit_bytes=32 << 20
        ),
    )(*(pltpu.with_memory_space_constraint(a, pltpu.HBM) for a in arrays))
    out = (*out[:3], out[3].reshape(width), *out[4:])
    out = pl.pallas_call(
        store,
        out_shape=tuple(shape(o.shape, o.dtype) for o in out),
        in_specs=[vmem] * 8,
        out_specs=(hbm,) * 8,
        scratch_shapes=[pltpu.SemaphoreType.DMA((8,))],
        compiler_params=pltpu.CompilerParams(vmem_limit_bytes=8 << 20),
    )(*(pltpu.with_memory_space_constraint(o, pltpu.VMEM) for o in out))
    return (*out[:7], out[7].reshape(ROWS))


def solution(mesh):
    return jax.shard_map(
        body,
        mesh=mesh,
        in_specs=(
            P("replica", None, "model"),
            P("replica", None, "model"),
            P("replica", "model", None),
            P("replica", None),
            P("replica", "model"),
            P("replica", "model"),
            P("model", "replica"),
            P("replica"),
        ),
        out_specs=(
            P(None, "model"),
            P(None, "model"),
            P("model", None),
            P(),
            P("replica", "model"),
            P("replica", "model"),
            P("model", "replica"),
            P("replica"),
        ),
        check_vma=False,
    )
```

time: 75.2 us -> 73.8 us (0.981)
  Pallas kernels: 73.9 us -> 73.1 us
    pallas_call x1, Pallas kernels: 71.5 us -> 70.6 us  [body(): pl.pallas_call(functools.partial(kernel, replicas, models), out_shape=(sh...]
where the time goes in v3:
time: 73.8 us; the launch traced here: 73.7 us
  Pallas kernels  73.1 us (99%)
    pallas_call x1, Pallas kernels, body(): pl.pallas_call(functools.partial(kernel, replicas, models), out_shape=(sh...  70.6 us
    pallas_call x1, Pallas kernels, body(): pl.pallas_call(store, out_shape=tuple((shape(o.shape, o.dtype) for o in o...  2.43 us

profile of v3, /device:TPU:1, one launch (start us, length us, event | category | flops | bytes accessed | tf_op | source)
XLA Modules:
  0.0 73.7 jit_solution(9213911053758352953)
XLA Ops:
  0.6 70.6 %shard_map.143 = (bf16[2048,384]{1,0:T(8,128)(2,1)S(1)}, bf16[2048,384]{1,0:T(8,128)(2,1)S(1)}, bf16[384,2048]{1,0:T(8,128)(2,1)S(1)}, bf16[2048]{0:T(1024)(128)...) custom-call(f32[1,2048,384]{2,1,0:T(8,128)} %refs_0_.1, ...), custom_call_target="tpu_custom_call" | custom-call | tf_op jit(solution)/shard_map/pallas_call | solution.py:501
  71.3 2.4 %shard_map.144 = (bf16[2048,384]{1,0:T(8,128)(2,1)}, bf16[2048,384]{1,0:T(8,128)(2,1)}, bf16[384,2048]{1,0:T(8,128)(2,1)}, bf16[2048]{0:T(1024)(128)(2,1)}, f32[...) custom-call(bf16[2048,384]{1,0:T(8,128)(2,1)S(1)} %get-tuple-element.24.refs_0_, ...), custom_call_target="tpu_custom_call" | custom-call | tf_op jit(solution)/shard_map/pallas_call | solution.py:542

commit v4 on v3

v4 whole, which is shorter than its diff:
```python
import functools

import jax
import jax.numpy as jnp
from jax import lax
from jax.experimental import pallas as pl
from jax.experimental.pallas import tpu as pltpu
from jax.sharding import PartitionSpec as P

MESH = pl.DeviceIdType.MESH
LEARN_RATE = 0.5
EPS = 1e-06
ROWS = 128
XS = 4
SENDS, RECVS = 34, 80


class Copies:
    def __init__(self, send, recv):
        self.send, self.recv, self.sends, self.recvs = send, recv, {}, {}

    def start(self, src, dst, target, sent, got):
        pltpu.make_async_remote_copy(
            src_ref=src,
            dst_ref=dst,
            send_sem=self.send.at[self.sends.setdefault(sent, len(self.sends))],
            recv_sem=self.recv.at[self.recvs.setdefault(got, len(self.recvs))],
            device_id=target,
            device_id_type=MESH,
        ).start()

    def gone(self, sent, size):
        pltpu.make_async_copy(size, size, self.send.at[self.sends[sent]]).wait()

    def here(self, got, size):
        pltpu.make_async_copy(size, size, self.recv.at[self.recvs[got]]).wait()


class Matrix:
    def __init__(self, by_rows, slope, param, half, new, s, r, p):
        self.by_rows, self.slope, self.param, self.half, self.new = by_rows, slope, param, half, new
        self.s, self.r, self.p = s, r, p

    def share(self, ref, index):
        at = pl.ds(pl.multiple_of(index * ROWS, ROWS), ROWS)
        return ref.at[at, :] if self.by_rows else ref.at[:, at]


class Tensor:
    def __init__(self, name, whole, x_first, direct, low, rows, x_in, y, src, nm):
        self.name, self.whole, self.x_first, self.direct = name, whole, x_first, direct
        self.low, self.rows, self.x_in, self.y, self.src, self.nm = low, rows, x_in, y, src, nm
        self.by_rows = whole.by_rows
        self.p = whole.p.at[pl.ds(low, rows)]
        self.new = whole.new.at[pl.ds(low, rows)]

    def blocks(self, count):
        if self.by_rows:
            return self.whole.half.at[pl.ds(0, count * self.rows), :]
        return self.whole.half.at[:, pl.ds(0, count * ROWS)]

    def sums(self, y, x):
        return self.whole.s.at[y, x, pl.ds(self.low, self.rows)]

    def block(self, index):
        return self.part(index, 0, self.rows)

    def part(self, index, at, rows):
        at = self.low + at
        if self.by_rows:
            at = pl.ds(pl.multiple_of(index * ROWS + at, rows), rows)
            return self.whole.half.at[at, :]
        return self.whole.half.at[pl.ds(at, rows), pl.ds(pl.multiple_of(index * ROWS, ROWS), ROWS)]

    def item(self, yh, h, x):
        if self.x_first:
            return self.sums(h, x)
        size = self.rows // 2
        return self.whole.s.at[yh, x, pl.ds(self.low + h * size, size)]

    def squares(self, value):
        value = value * value
        if not self.by_rows:
            return jnp.sum(value, axis=0, keepdims=True)
        folded = value[:, :ROWS]
        for at in range(ROWS, value.shape[1], ROWS):
            folded = folded + value[:, at : at + ROWS]
        if self.rows < ROWS:
            folded = jnp.concatenate([folded, jnp.zeros_like(folded)], axis=0)
        return jnp.sum(folded.T, axis=0, keepdims=True)


class Vector:
    name, x_first = "n", True

    def __init__(self, s, x_in, y):
        self.s, self.x_in, self.y = s, x_in, y

    def item(self, yh, h, x):
        return self.s.at[h, x]


def add(into, *others):
    value = into[...]
    for other in others:
        value = value + other[...]
    into[...] = value


def kernel(replicas, models, *refs):
    (sg, su, sd, sn, pg, pu, pd, pn), refs = refs[:8], refs[8:]
    (hg, hu, hd, hn, ng, nu, nd, nn), refs = refs[:8], refs[8:]
    my, refs = Matrix(True, sg, pg, hg, ng, *refs[:3]), refs[3:]
    mb, refs = Matrix(True, su, pu, hu, nu, *refs[:3]), refs[3:]
    ma, refs = Matrix(False, sd, pd, hd, nd, *refs[:3]), refs[3:]
    half = ROWS // 2
    deep = ma.p.shape[0]
    ta = Tensor("a", ma, True, False, 0, deep, None, None, *refs[2:4])
    a1 = Tensor("a1", ma, True, False, 0, deep // 2, *refs[:2], None, None)
    refs = refs[4:]
    a2 = Tensor("a2", ma, True, False, deep // 2, deep // 2, *refs[:2], None, None)
    refs = refs[2:]
    b1, refs = Tensor("b1", mb, True, False, 0, half, *refs[:4]), refs[4:]
    b2, refs = Tensor("b2", mb, True, False, half, half, *refs[:4]), refs[4:]
    y1, refs = Tensor("y1", my, False, True, 0, half, refs[0], None, *refs[1:3]), refs[3:]
    y2, refs = Tensor("y2", my, False, True, half, half, refs[0], None, *refs[1:3]), refs[3:]
    y_in, refs = refs[0], refs[1:]
    tn, refs = Vector(*refs[:3]), refs[3:]
    gain, pn_here, sn_here, sn_other, a_out, y_out, refs = *refs[:6], refs[6:]
    local_sem, send_sem, recv_sem, hop_sem = refs

    r = lax.axis_index("replica")
    m = lax.axis_index("model")
    core = r % 2
    x = (r // 2) % XS
    yh = r // (2 * XS)
    yo = 1 - yh
    xr, xl, x2 = (x + 1) % XS, (x + XS - 1) % XS, (x + 2) % XS

    def owner(y, xx, c):
        return (y * XS + xx) * 2 + c

    def device(y, xx, c):
        return {"replica": owner(y, xx, c), "model": m}

    right, left = device(yh, xr, core), device(yh, xl, core)
    across, partner = device(yo, x, core), device(yh, x, 1 - core)
    beyond = device(yh, x2, core)
    net = Copies(send_sem, recv_sem)
    others = [{"replica": r, "model": (m + k) % models} for k in range(1, models)]
    zs = models // 2
    z, yl = m // 2, m % 2
    up = {"replica": r, "model": (z + 1) % zs * 2 + yl}
    down = {"replica": r, "model": (z + zs - 1) % zs * 2 + yl}
    beside = {"replica": r, "model": z * 2 + 1 - yl}

    def signal(sem, *peers):
        for peer in peers:
            pl.semaphore_signal(sem, inc=1, device_id=peer, device_id_type=MESH)

    barrier = pltpu.get_barrier_semaphore()
    signal(barrier, partner, right, left, across, up, down, beside)

    order = [("af", ma, 0, x2), ("af", ma, 1, x2), ("y0", my, yo, x2)]
    order += [("an", ma, 1, xr), ("an", ma, 0, xl), ("y1", my, yo, xr)]
    order += [("ar", ma, 0, xr), ("ar", ma, 1, xl), ("y2", my, yo, xl)]
    order += [("bf", mb, 0, x2), ("bf", mb, 1, x2), ("y3", my, yo, x)]
    order += [("yx2", my, yh, x2), ("bn", mb, 1, xr), ("bn", mb, 0, xl)]
    order += [("br", mb, 0, xr), ("br", mb, 1, xl), ("yx", my, yh, xr)]
    order += [("yx", my, yh, xl), ("ao", ma, 0, x), ("ao", ma, 1, x)]
    order += [("bo", mb, 0, x), ("bo", mb, 1, x), ("yo", my, yh, x)]
    def load(src, dst, sem):
        pltpu.make_async_copy(src, dst, local_sem.at[sem]).start()

    def loaded(ref, sem):
        pltpu.make_async_copy(ref, ref, local_sem.at[sem]).wait()

    early, outs = {"af": ma, "an": ma, "y0": my}, {}
    for i, (tag, t, y, xx) in enumerate(order):
        if tag in early:
            n = len([k for k in outs if order[k][1] is t])
            outs[i] = (a_out if t is ma else y_out).at[n]
            load(t.share(t.slope.at[0], owner(y, xx, 1 - core)), outs[i], 0 if t is ma else 1)
    for tag, t, y, xx in order:
        load(t.share(t.slope.at[0], owner(y, xx, core)), t.s.at[y, xx], (ma, my, mb).index(t) + 2)
    for i, t in enumerate((ma, mb, my)):
        load(t.param, t.p, 5 + i)
    load(pn, pn_here, 8)
    load(sn, sn_here, 9)
    loaded(a_out, 0)
    loaded(y_out, 1)
    pl.semaphore_wait(barrier, 7)

    for i, (tag, t, y, xx) in enumerate(order):
        src = outs[i] if i in outs else t.share(t.slope.at[0], owner(y, xx, 1 - core))
        net.start(src, t.r.at[y, xx], partner, "swap" + "amby"[(ma, mb, my).index(t)], tag)
        if tag == "y2":
            net.start(sn, sn_other, partner, "sn", "sn")
            signal(hop_sem.at[0], up, down)
    for i, t in enumerate((ma, my, mb)):
        loaded(t.s, 2 + i)

    taken = [0]

    def take(tag):
        end = max(i for i, entry in enumerate(order) if entry[0] == tag) + 1
        for i in range(taken[0], end):
            name, t, y, xx = order[i]
            group = [j for j, entry in enumerate(order) if entry[0] == name]
            if i == group[0]:
                net.here(name, t.s.at[0, pl.ds(0, len(group))])
            add(t.s.at[y, xx], t.r.at[y, xx])
        taken[0] = max(taken[0], end)

    def x_send(t, h, xx, slot, target, stage):
        net.start(t.item(yh, h, xx), t.x_in.at[slot], target, t.name + "x", t.name + stage)

    def far(t):
        x_send(t, 0, x2, 0, right, "far")
        x_send(t, 1, x2, 1, left, "far")

    def near(t):
        x_send(t, 0, xl, 2, left, "near")
        x_send(t, 1, xr, 3, right, "near")

    def relay(t):
        net.here(t.name + "far", t.x_in.at[pl.ds(0, 2)])
        add(t.item(yh, 0, xr), t.x_in.at[0])
        x_send(t, 0, xr, 4, right, "near")
        add(t.item(yh, 1, xl), t.x_in.at[1])
        x_send(t, 1, xl, 5, left, "near")

    def settle(t):
        net.here(t.name + "near", t.x_in.at[pl.ds(2, 4)])
        for h in (0, 1):
            add(t.item(yh, h, x), t.x_in.at[2 + h], t.x_in.at[4 + h])

    def finish(t, extra=()):
        own = t.sums(yh, x)
        value = own[...]
        for e in extra:
            value = value + e[...]
        value = value * (replicas**-0.5)
        own[...] = value
        t.src[0:1, :] = t.squares(value)
        for k, peer in enumerate(others, 1):
            net.start(t.src, t.nm.at[k], peer, t.name + "norm", t.name + "norm")

    def update(t):
        total = t.src[...]
        net.here(t.name + "norm", t.nm.at[pl.ds(1, models - 1)])
        for k in range(1, models):
            total = total + t.nm[k]
        ratio = jnp.sqrt(total[1:2]) * lax.rsqrt(total[0:1] + EPS)
        if t.by_rows:
            ratio = jnp.broadcast_to(ratio, (ROWS, ROWS)).T[: t.rows]
            ratio = jnp.concatenate([ratio] * (t.p.shape[1] // ROWS), axis=1)
        new = t.p[...] - LEARN_RATE * (t.sums(yh, x)[...] * ratio)
        t.new[...] = new
        t.block(owner(yh, x, core))[...] = new.astype(jnp.bfloat16)

    def spread(t, y, xx, target, got):
        block = t.block(owner(y, xx, core))
        net.start(block, block, target, t.name + "half", t.name + got)

    def hand(t, y, xx):
        block = t.block(owner(y, xx, core))
        net.start(block, block, partner, t.name + "hand", t.name + "hand")

    def around(t, y, got):
        spread(t, y, x, right, got)
        spread(t, y, x, left, got)
        if t.direct:
            spread(t, y, x, beyond, got + "2")

    def wait(t, got, count):
        net.here(t.name + got, t.blocks(count))

    def rise(t):
        net.start(t.sums(yo, x), t.y, across, t.name + "y", t.name + "y")

    def risen(t):
        net.here(t.name + "y", t.y)
        finish(t, (t.y,))

    def y_send(xx, j):
        net.start(my.s.at[yo, xx], y_in.at[j], across, "y", "in%d" % j)

    def fold(xx, j):
        net.here("in%d" % j, y_in.at[j])
        add(my.s.at[yh, xx], y_in.at[j])

    def publish(t):
        update(t)
        spread(t, yh, x, across, "up")
        hand(t, yh, x)

    def second(t):
        wait(t, "up", 1)
        around(t, yo, "oth")
        hand(t, yo, x)

    def pass_own(t):
        wait(t, "own", 2)
        if not t.direct:
            spread(t, yh, xl, right, "own2")
        hand(t, yh, xl)
        hand(t, yh, xr)

    def pass_oth(t):
        wait(t, "oth", 2)
        if not t.direct:
            spread(t, yo, xr, left, "oth2")
        hand(t, yo, xl)
        hand(t, yo, xr)

    def last(t, y, got):
        wait(t, got, 1)
        hand(t, y, x2)

    def publish_y(t):
        update(t)
        around(t, yh, "own")
        spread(t, yh, x, across, "up0")
        hand(t, yh, x)

    def climb(t):
        wait(t, "own", 2)
        spread(t, yh, xl, across, "up1")
        spread(t, yh, xr, across, "up1")
        hand(t, yh, xl)
        hand(t, yh, xr)

    def climb2(t):
        wait(t, "own2", 1)
        spread(t, yh, x2, across, "up2")
        hand(t, yh, x2)

    def tell(y, target, got):
        row = gain.at[core, y * XS + x]
        net.start(row, row, target, "tell", got)

    def told(got, count):
        net.here(got, gain.at[0, pl.ds(0, count)])

    take("af")
    far(a1)
    far(a2)
    take("y0")
    y_send(x2, 0)
    take("an")
    near(a1)
    near(a2)
    take("y1")
    y_send(xr, 1)
    take("ar")
    take("y2")
    y_send(xl, 2)
    for i, t in enumerate((ma, mb, my)):
        loaded(t.p, 5 + i)
    for t in (ta, b1, b2, y1, y2):
        t.src[1:2, :] = t.squares(t.p[...])
    take("bf")
    relay(a1)
    take("yx2")
    relay(a2)
    loaded(sn_here, 9)
    net.here("sn", sn_other)
    for y in (0, 1):
        for xx in range(XS):
            at = pl.ds(pl.multiple_of(owner(y, xx, core) * ROWS, ROWS), ROWS)
            tn.s[y, xx] = sn_here[0:1, at] + sn_other[0:1, at]
    far(tn)
    near(tn)
    far(b1)
    far(b2)
    pl.semaphore_wait(hop_sem.at[0], 2)
    signal(hop_sem.at[1], up, down)
    take("bn")
    near(b1)
    fold(x2, 0)
    pl.semaphore_wait(hop_sem.at[1], 2)
    signal(hop_sem.at[2], up, down)
    take("yo")
    pl.semaphore_wait(hop_sem.at[2], 2)
    signal(hop_sem.at[3], beside)
    fold(xr, 1)
    net.gone("sn", sn_other)
    for name, t in (("swapa", ma), ("swapm", mb), ("swapb", my)):
        net.gone(name, t.s)
    settle(a1)
    rise(a1)
    settle(a2)
    rise(a2)
    y_send(x, 3)
    relay(tn)
    fold(xl, 2)
    relay(b1)
    near(b2)
    relay(b2)
    far(y1)
    far(y2)
    near(y1)
    near(y2)
    pl.semaphore_wait(hop_sem.at[3], 1)
    for t in (a1, a2):
        net.gone(t.name + "x", t.x_in)
        net.here(t.name + "y", t.y)
        add(t.sums(yh, x), t.y)
    finish(ta)
    settle(b1)
    rise(b1)
    fold(x, 3)
    publish(ta)
    settle(b2)
    rise(b2)
    relay(y1)
    risen(b1)
    relay(y2)
    around(ta, yh, "own")
    settle(tn)
    net.start(tn.s.at[yo, x], tn.y, across, "ny", "ny")
    second(ta)
    risen(b2)
    settle(y1)
    finish(y1)
    settle(y2)
    finish(y2)
    publish(b1)
    around(b1, yh, "own")
    loaded(pn_here, 8)
    net.here("ny", tn.y)
    add(tn.s.at[yh, x], tn.y)
    gain[core, yh * XS + x] = pn_here[...] - LEARN_RATE * (tn.s[yh, x] * (replicas**-0.5))
    nn[...] = gain[core, yh * XS + x]
    tell(yh, across, "nup")
    for target, got in ((right, "nown"), (left, "nown"), (beyond, "nown2")):
        tell(yh, target, got)
    pass_own(ta)
    for t in (a1, a2, b1, b2):
        net.gone(t.name + "y", t.y)
    net.gone("ny", tn.y)
    net.gone("y", y_in)
    net.gone("nx", tn.x_in)
    publish(b2)
    publish_y(y1)
    publish_y(y2)
    around(b2, yh, "own")
    pass_oth(ta)
    second(b1)
    pass_own(b1)
    told("nup", 1)
    for target, got in ((right, "noth"), (left, "noth"), (beyond, "noth2")):
        tell(yo, target, got)
    for t in (ta, b1, b2, y1, y2):
        net.gone(t.name + "norm", t.nm.at[pl.ds(1, models - 1)])
        if t is not ta:
            net.gone(t.name + "x", t.x_in)
    climb(y1)
    second(b2)
    climb2(y1)
    climb(y2)
    climb2(y2)
    pass_own(b2)
    pass_oth(b1)
    last(ta, yh, "own2")
    last(ta, yo, "oth2")
    told("nown", 2)
    told("nown2", 1)
    told("noth", 2)
    told("noth2", 1)
    net.start(gain.at[core], gain.at[core], partner, "nhand", "nhand")
    pass_oth(b2)
    for t in (y1, y2):
        wait(t, "up0", 1)
        hand(t, yo, x)
    net.here("nhand", gain.at[core])
    for y in (0, 1):
        for xx in range(XS):
            for c in (0, 1):
                at = owner(y, xx, c) * ROWS
                hn[at : at + ROWS] = gain[c, y * XS + xx, 0, :].astype(jnp.bfloat16)
    net.gone("nhand", gain.at[core])
    net.gone("tell", gain.at[0, pl.ds(0, 7)])
    net.gone("ahalf", ta.blocks(7))
    last(b1, yh, "own2")
    net.here("ahand", ta.blocks(8))
    net.gone("ahand", ta.blocks(8))

    def top(t):
        wait(t, "up1", 2)
        hand(t, yo, xl)
        hand(t, yo, xr)

    top(y1)
    last(b1, yo, "oth2")
    last(b2, yh, "own2")
    top(y2)
    last(y1, yo, "up2")
    last(b2, yo, "oth2")
    last(y2, yo, "up2")
    for t in (b1, y1, b2, y2):
        net.here(t.name + "hand", t.blocks(8))
        net.gone(t.name + "half", t.blocks(7))
        net.gone(t.name + "hand", t.blocks(8))


def store(*refs):
    copies = [
        pltpu.make_async_copy(refs[i], refs[8 + i], refs[16].at[i]) for i in range(8)
    ]
    for copy in copies:
        copy.start()
    for copy in copies:
        copy.wait()


def body(sg, su, sd, sn, pg, pu, pd, pn):
    arrays = (sg, su, sd, sn, pg, pu, pd, pn.reshape(1, ROWS))
    replicas, models = lax.axis_size("replica"), lax.axis_size("model")
    width, cols = sg.shape[1:]
    f32, bf16 = jnp.float32, jnp.bfloat16

    def matrix(share):
        sums = pltpu.VMEM((2, XS, *share), f32)
        return [sums, sums, pltpu.VMEM(share, f32)]

    def scratch(block, x_first):
        item = block if x_first else (block[0] // 2, block[1])
        arrived = [pltpu.VMEM((6, *item), f32)] + [pltpu.VMEM(block, f32)] * x_first
        return arrived + [pltpu.VMEM((2, ROWS), f32), pltpu.VMEM((models, 2, ROWS), f32)]

    vmem = pl.BlockSpec(memory_space=pltpu.VMEM)
    hbm = pl.BlockSpec(memory_space=pltpu.HBM)
    shape = jax.ShapeDtypeStruct
    out = pl.pallas_call(
        functools.partial(kernel, replicas, models),
        out_shape=(
            shape((width, cols), bf16),
            shape((width, cols), bf16),
            shape((cols, width), bf16),
            shape((width,), bf16),
            shape((ROWS, cols), f32),
            shape((ROWS, cols), f32),
            shape((cols, ROWS), f32),
            shape((1, ROWS), f32),
        ),
        in_specs=[hbm] * 8,
        out_specs=(vmem,) * 8,
        scratch_shapes=[
            *matrix((ROWS, cols)),
            *matrix((ROWS, cols)),
            *matrix((cols, ROWS)),
            *scratch((cols // 2, ROWS), True),
            *scratch((cols // 2, ROWS), True)[:2],
            *scratch((ROWS // 2, cols), True),
            *scratch((ROWS // 2, cols), True),
            *scratch((ROWS // 2, cols), False),
            *scratch((ROWS // 2, cols), False),
            pltpu.VMEM((XS, ROWS, cols), f32),
            pltpu.VMEM((2, XS, 1, ROWS), f32),
            pltpu.VMEM((6, 1, ROWS), f32),
            pltpu.VMEM((1, ROWS), f32),
            pltpu.VMEM((2, 2 * XS, 1, ROWS), f32),
            pltpu.VMEM((1, ROWS), f32),
            pltpu.VMEM((1, width), f32),
            pltpu.VMEM((1, width), f32),
            pltpu.VMEM((4, cols, ROWS), f32),
            pltpu.VMEM((1, ROWS, cols), f32),
            pltpu.SemaphoreType.DMA((10,)),
            pltpu.SemaphoreType.DMA((SENDS,)),
            pltpu.SemaphoreType.DMA((RECVS,)),
            pltpu.SemaphoreType.REGULAR((4,)),
        ],
        compiler_params=pltpu.CompilerParams(
            collective_id=0, has_side_effects=True, vmem_limit_bytes=32 << 20
        ),
    )(*(pltpu.with_memory_space_constraint(a, pltpu.HBM) for a in arrays))
    out = (*out[:3], out[3].reshape(width), *out[4:])
    out = pl.pallas_call(
        store,
        out_shape=tuple(shape(o.shape, o.dtype) for o in out),
        in_specs=[vmem] * 8,
        out_specs=(hbm,) * 8,
        scratch_shapes=[pltpu.SemaphoreType.DMA((8,))],
        compiler_params=pltpu.CompilerParams(vmem_limit_bytes=8 << 20),
    )(*(pltpu.with_memory_space_constraint(o, pltpu.VMEM) for o in out))
    return (*out[:7], out[7].reshape(ROWS))


def solution(mesh):
    return jax.shard_map(
        body,
        mesh=mesh,
        in_specs=(
            P("replica", None, "model"),
            P("replica", None, "model"),
            P("replica", "model", None),
            P("replica", None),
            P("replica", "model"),
            P("replica", "model"),
            P("model", "replica"),
            P("replica"),
        ),
        out_specs=(
            P(None, "model"),
            P(None, "model"),
            P("model", None),
            P(),
            P("replica", "model"),
            P("replica", "model"),
            P("model", "replica"),
            P("replica"),
        ),
        check_vma=False,
    )
```

time: 73.8 us -> 68.8 us (0.932)
  Pallas kernels: 73.1 us -> 68.1 us
    pallas_call x1, Pallas kernels: 70.6 us -> 65.7 us  [body(): pl.pallas_call(functools.partial(kernel, replicas, models), out_shape=(sh...]
where the time goes in v4:
time: 68.8 us
  Pallas kernels  68.1 us (99%)
    pallas_call x1, Pallas kernels, body(): pl.pallas_call(functools.partial(kernel, replicas, models), out_shape=(sh...  65.7 us
    pallas_call x1, Pallas kernels, body(): pl.pallas_call(store, out_shape=tuple((shape(o.shape, o.dtype) for o in o...  2.43 us

profile of v4, /device:TPU:1, one launch (start us, length us, event | category | flops | bytes accessed | tf_op | source)
XLA Modules:
  0.0 68.8 jit_solution(15221783087820122149)
XLA Ops:
  0.6 65.7 %shard_map.143 = (bf16[2048,384]{1,0:T(8,128)(2,1)S(1)}, bf16[2048,384]{1,0:T(8,128)(2,1)S(1)}, bf16[384,2048]{1,0:T(8,128)(2,1)S(1)}, bf16[2048]{0:T(1024)(128)...) custom-call(f32[1,2048,384]{2,1,0:T(8,128)} %refs_0_.1, ...), custom_call_target="tpu_custom_call" | custom-call | tf_op jit(solution)/shard_map/pallas_call | solution.py:536
  66.3 2.4 %shard_map.144 = (bf16[2048,384]{1,0:T(8,128)(2,1)}, bf16[2048,384]{1,0:T(8,128)(2,1)}, bf16[384,2048]{1,0:T(8,128)(2,1)}, bf16[2048]{0:T(1024)(128)(2,1)}, f32[...) custom-call(bf16[2048,384]{1,0:T(8,128)(2,1)S(1)} %get-tuple-element.24.refs_0_, ...), custom_call_target="tpu_custom_call" | custom-call | tf_op jit(solution)/shard_map/pallas_call | solution.py:580

commit v5 on v4

--- a/solution.py
+++ b/solution.py
@@ -12,7 +12,8 @@
 EPS = 1e-06
 ROWS = 128
 XS = 4
-SENDS, RECVS = 34, 80
+TURNED = 16
+SENDS, RECVS = 36, 86
 
 
 class Copies:
@@ -121,7 +122,12 @@
     a2 = Tensor("a2", ma, True, False, deep // 2, deep // 2, *refs[:2], None, None)
     refs = refs[2:]
     b1, refs = Tensor("b1", mb, True, False, 0, half, *refs[:4]), refs[4:]
-    b2, refs = Tensor("b2", mb, True, False, half, half, *refs[:4]), refs[4:]
+    straight = half - TURNED
+    b2 = Tensor("b2", mb, True, False, half, half, None, None, *refs[2:4])
+    b3 = Tensor("b3", mb, True, False, half, straight, *refs[:2], None, None)
+    refs = refs[4:]
+    b4 = Tensor("b4", mb, False, False, half + straight, TURNED, refs[0], None, None, None)
+    b4_in, refs = refs[1], refs[2:]
     y1, refs = Tensor("y1", my, False, True, 0, half, refs[0], None, *refs[1:3]), refs[3:]
     y2, refs = Tensor("y2", my, False, True, half, half, refs[0], None, *refs[1:3]), refs[3:]
     y_in, refs = refs[0], refs[1:]
@@ -289,6 +295,13 @@
     def fold(xx, j):
         net.here("in%d" % j, y_in.at[j])
         add(my.s.at[yh, xx], y_in.at[j])
+
+    def turn(xx, j):
+        net.start(b4.sums(yo, xx), b4_in.at[j], across, "b4y", "b4in%d" % j)
+
+    def turned(xx, j):
+        net.here("b4in%d" % j, b4_in.at[j])
+        add(b4.sums(yh, xx), b4_in.at[j])
 
     def publish(t):
         update(t)
@@ -373,7 +386,7 @@
     far(tn)
     near(tn)
     far(b1)
-    far(b2)
+    far(b3)
     pl.semaphore_wait(hop_sem.at[0], 2)
     signal(hop_sem.at[1], up, down)
     take("bn")
@@ -384,6 +397,9 @@
     take("yo")
     pl.semaphore_wait(hop_sem.at[2], 2)
     signal(hop_sem.at[3], beside)
+    turn(x2, 0)
+    turn(xr, 1)
+    turn(xl, 2)
     fold(xr, 1)
     net.gone("sn", sn_other)
     for name, t in (("swapa", ma), ("swapm", mb), ("swapb", my)):
@@ -393,11 +409,17 @@
     settle(a2)
     rise(a2)
     y_send(x, 3)
+    turn(x, 3)
     relay(tn)
     fold(xl, 2)
     relay(b1)
-    near(b2)
-    relay(b2)
+    near(b3)
+    turned(x2, 0)
+    far(b4)
+    relay(b3)
+    turned(xr, 1)
+    turned(xl, 2)
+    near(b4)
     far(y1)
     far(y2)
     near(y1)
@@ -410,22 +432,27 @@
     finish(ta)
     settle(b1)
     rise(b1)
-    fold(x, 3)
     publish(ta)
-    settle(b2)
-    rise(b2)
+    settle(b3)
+    rise(b3)
+    relay(b4)
     relay(y1)
     risen(b1)
     relay(y2)
     around(ta, yh, "own")
     settle(tn)
     net.start(tn.s.at[yo, x], tn.y, across, "ny", "ny")
-    second(ta)
-    risen(b2)
+    fold(x, 3)
+    turned(x, 3)
+    settle(b4)
+    net.here("b3y", b3.y)
+    add(b3.sums(yh, x), b3.y)
+    finish(b2)
     settle(y1)
     finish(y1)
     settle(y2)
     finish(y2)
+    second(ta)
     publish(b1)
     around(b1, yh, "own")
     loaded(pn_here, 8)
@@ -437,8 +464,9 @@
     for target, got in ((right, "nown"), (left, "nown"), (beyond, "nown2")):
         tell(yh, target, got)
     pass_own(ta)
-    for t in (a1, a2, b1, b2):
+    for t in (a1, a2, b1, b3):
         net.gone(t.name + "y", t.y)
+    net.gone("b4y", b4_in)
     net.gone("ny", tn.y)
     net.gone("y", y_in)
     net.gone("nx", tn.x_in)
@@ -454,8 +482,8 @@
         tell(yo, target, got)
     for t in (ta, b1, b2, y1, y2):
         net.gone(t.name + "norm", t.nm.at[pl.ds(1, models - 1)])
-        if t is not ta:
-            net.gone(t.name + "x", t.x_in)
+    for t in (b1, b3, b4, y1, y2):
+        net.gone(t.name + "x", t.x_in)
     climb(y1)
     second(b2)
     climb2(y1)
@@ -554,7 +582,9 @@
             *scratch((cols // 2, ROWS), True),
             *scratch((cols // 2, ROWS), True)[:2],
             *scratch((ROWS // 2, cols), True),
-            *scratch((ROWS // 2, cols), True),
+            *scratch((ROWS // 2 - TURNED, cols), True),
+            pltpu.VMEM((6, TURNED // 2, cols), f32),
+            pltpu.VMEM((XS, TURNED, cols), f32),
             *scratch((ROWS // 2, cols), False),
             *scratch((ROWS // 2, cols), False),
             pltpu.VMEM((XS, ROWS, cols), f32),

time: 68.8 us -> 68.3 us (level)
  no operation moved by 1% of the time
where the time goes in v5:
time: 68.3 us
  Pallas kernels  67.6 us (99%)
    pallas_call x1, Pallas kernels, body(): pl.pallas_call(functools.partial(kernel, replicas, models), out_shape=(sh...  65.2 us
    pallas_call x1, Pallas kernels, body(): pl.pallas_call(store, out_shape=tuple((shape(o.shape, o.dtype) for o in o...  2.43 us

profile of v5, /device:TPU:1, one launch (start us, length us, event | category | flops | bytes accessed | tf_op | source)
XLA Modules:
  0.0 68.3 jit_solution(13157312588240312803)
XLA Ops:
  0.6 65.2 %shard_map.143 = (bf16[2048,384]{1,0:T(8,128)(2,1)S(1)}, bf16[2048,384]{1,0:T(8,128)(2,1)S(1)}, bf16[384,2048]{1,0:T(8,128)(2,1)S(1)}, bf16[2048]{0:T(1024)(128)...) custom-call(f32[1,2048,384]{2,1,0:T(8,128)} %refs_0_.1, ...), custom_call_target="tpu_custom_call" | custom-call | tf_op jit(solution)/shard_map/pallas_call | solution.py:564
  65.8 2.4 %shard_map.144 = (bf16[2048,384]{1,0:T(8,128)(2,1)}, bf16[2048,384]{1,0:T(8,128)(2,1)}, bf16[384,2048]{1,0:T(8,128)(2,1)}, bf16[2048]{0:T(1024)(128)(2,1)}, f32[...) custom-call(bf16[2048,384]{1,0:T(8,128)(2,1)S(1)} %get-tuple-element.24.refs_0_, ...), custom_call_target="tpu_custom_call" | custom-call | tf_op jit(solution)/shard_map/pallas_call | solution.py:610

commit v6 on v5

--- a/solution.py
+++ b/solution.py
@@ -484,8 +484,8 @@
         net.gone(t.name + "norm", t.nm.at[pl.ds(1, models - 1)])
     for t in (b1, b3, b4, y1, y2):
         net.gone(t.name + "x", t.x_in)
+    second(b2)
     climb(y1)
-    second(b2)
     climb2(y1)
     climb(y2)
     climb2(y2)

time: 68.3 us -> 68.3 us (level)
  no operation moved by 1% of the time
where the time goes in v6:
time: 68.3 us
  Pallas kernels  67.6 us (99%)
    pallas_call x1, Pallas kernels, body(): pl.pallas_call(functools.partial(kernel, replicas, models), out_shape=(sh...  65.2 us
    pallas_call x1, Pallas kernels, body(): pl.pallas_call(store, out_shape=tuple((shape(o.shape, o.dtype) for o in o...  2.43 us

profile of v6, /device:TPU:1, one launch (start us, length us, event | category | flops | bytes accessed | tf_op | source)
XLA Modules:
  0.0 68.3 jit_solution(16589702591403374274)
XLA Ops:
  0.6 65.2 %shard_map.143 = (bf16[2048,384]{1,0:T(8,128)(2,1)S(1)}, bf16[2048,384]{1,0:T(8,128)(2,1)S(1)}, bf16[384,2048]{1,0:T(8,128)(2,1)S(1)}, bf16[2048]{0:T(1024)(128)...) custom-call(f32[1,2048,384]{2,1,0:T(8,128)} %refs_0_.1, ...), custom_call_target="tpu_custom_call" | custom-call | tf_op jit(solution)/shard_map/pallas_call | solution.py:564
  65.8 2.4 %shard_map.144 = (bf16[2048,384]{1,0:T(8,128)(2,1)}, bf16[2048,384]{1,0:T(8,128)(2,1)}, bf16[384,2048]{1,0:T(8,128)(2,1)}, bf16[2048]{0:T(1024)(128)(2,1)}, f32[...) custom-call(bf16[2048,384]{1,0:T(8,128)(2,1)S(1)} %get-tuple-element.24.refs_0_, ...), custom_call_target="tpu_custom_call" | custom-call | tf_op jit(solution)/shard_map/pallas_call | solution.py:610
